TPU v7x, 32 devices: a whole 2x2x4 slice. The times are simulated.
32 devices in a mesh: row: 16 (over z, y, x), col: 2 (over core).
Axes of the slice: x: 2, y: 2, z: 4, core: 2. Of those that a mesh axis runs over, the one named last changes fastest.
Arguments:
- eri_cols: float32 [8192, 512], P('row'), as said below
- old_factor: float32 [8192, 1024], P('row', 'col')
- residual_diag: float32 [8192], P('row'), as said below
- pivots: int32 [4, 128], replicated, may hold values from 0 to 8191, as said below
- row_ids: int32 [8192], P('row'), may hold values from 0 to 8191, as said below
Outputs:
- panels: float32 [8192, 512], P('row')
- new_diag: float32 [8192], P('row')
Inputs may be any that keep to these rules, and one draw needn't show every extreme that they name: `pivots`: 512 distinct pair indices, each held by some stored row. `row_ids`: every pair index held by exactly one stored row. `eri_cols`: the pair matrix minus the earlier factor's product is symmetric positive definite on the pivots, with smallest eigenvalue 0.25 or more. `residual_diag`: the diagonal of the same residual matrix whose pivot columns eri_cols holds.
All inputs are finite; a program needn't handle non-finite values.
Results may differ from a plain program's by a relative error of at most 0.0003.
Values sent between devices are 32-bit elements; how exact they have to be, the bound alone decides.
A program may use at most 64 MiB of HBM per device.

v0:
```python
import functools
import jax
import jax.numpy as jnp
from jax import lax
from jax.experimental import pallas as pl
from jax.experimental.pallas import tpu as pltpu
from jax.sharding import PartitionSpec as P

ROWS_T = (((1,), (1,)), ((), ()))
SUB = 8


def split(x):
    hi = x.astype(jnp.bfloat16)
    return hi, (x - hi.astype(jnp.float32)).astype(jnp.bfloat16)


def dot_t(a, b):
    f = functools.partial(
        lax.dot_general, dimension_numbers=ROWS_T, preferred_element_type=jnp.float32
    )
    return f(a[0], b[0]) + (f(a[0], b[1]) + f(a[1], b[0]))


def inverse_factor(a):
    n = a.shape[0]
    groups = n // SUB
    row = lax.broadcasted_iota(jnp.int32, (SUB, n), 0)
    lane = lax.broadcasted_iota(jnp.int32, (SUB, n), 1)
    A = [a[SUB * i : SUB * i + SUB, :] for i in range(groups)]
    W = [jnp.where(lane == row + SUB * i, 1.0, 0.0) for i in range(groups)]
    out = []
    wide = lambda v: jnp.broadcast_to(v, (SUB, n))
    for g in range(groups):
        j = SUB * g
        C = [[wide(A[i][:, j + k : j + k + 1]) for k in range(SUB)] for i in range(g, groups)]
        D = [[wide(C[0][l][k : k + 1, :]) for l in range(k + 1)] for k in range(SUB)]
        r = [wide(A[g][k : k + 1, :]) for k in range(SUB)]
        w = [wide(W[g][k : k + 1, :]) for k in range(SUB)]
        inv, m = [], [[None] * SUB for _ in range(SUB)]
        done = jnp.zeros((SUB, n), jnp.float32)
        for k in range(SUB):
            root = lax.rsqrt(D[k][k])
            inv.append(root * root)
            done = jnp.where(row == k, w[k] * root, done)
            for i in range(k + 1, SUB):
                m[i][k] = D[i][k] * inv[k]
            for i in range(k + 1, SUB):
                for l in range(k + 1, i + 1):
                    D[i][l] = D[i][l] - m[i][k] * D[l][k]
                r[i] = r[i] - m[i][k] * r[k]
                w[i] = w[i] - m[i][k] * w[k]
        out.append(done)
        if g + 1 == groups:
            break
        s, t = [None] * SUB, [None] * SUB
        for k in reversed(range(SUB)):
            s[k], t[k] = r[k] * inv[k], w[k] * inv[k]
            for i in reversed(range(k + 1, SUB)):
                s[k] = s[k] - m[i][k] * s[i]
                t[k] = t[k] - m[i][k] * t[i]
        for i in range(g + 1, groups):
            c = C[i - g]
            for k in range(SUB):
                A[i] = A[i] - c[k] * s[k]
                W[i] = W[i] - c[k] * t[k]
    return jnp.concatenate(out, axis=0)


def factor_kernel(steps, pivot_ref, rows_ref, diag_ref, panel_ref, new_ref, work):
    piv = pivot_ref.shape[0]
    width = piv // steps
    work[:piv, :] = pivot_ref[...]
    work[piv:, :] = rows_ref[...]
    new_ref[...] = diag_ref[...]
    ones = jnp.ones((SUB, width), jnp.bfloat16)

    def step(s, carry):
        at = pl.ds(pl.multiple_of(s * width, width), width)
        inv = split(inverse_factor(work[at, at]))
        solved = dot_t(split(work[:, at]), inv)
        own = solved[piv:]
        panel_ref[:, at] = own
        hi, lo = split(own * own)
        f = functools.partial(
            lax.dot_general, dimension_numbers=ROWS_T, preferred_element_type=jnp.float32
        )
        new_ref[...] -= (f(ones, hi) + f(ones, lo))[:1]

        @pl.when(s < steps - 1)
        def _():
            both = split(solved)
            work[...] -= dot_t(both, (both[0][:piv], both[1][:piv]))

        return carry

    lax.fori_loop(0, steps, step, 0)


def factor(pivot_rows, reduced, diagonal, steps):
    piv, rows = pivot_rows.shape[0], reduced.shape[0]
    panels, new = pl.pallas_call(
        functools.partial(factor_kernel, steps),
        out_shape=(
            jax.ShapeDtypeStruct((rows, piv), jnp.float32),
            jax.ShapeDtypeStruct((1, rows), jnp.float32),
        ),
        in_specs=[pl.BlockSpec(memory_space=pltpu.VMEM)] * 3,
        out_specs=[pl.BlockSpec(memory_space=pltpu.VMEM)] * 2,
        scratch_shapes=[pltpu.VMEM((piv + rows, piv), jnp.float32)],
        compiler_params=pltpu.CompilerParams(vmem_limit_bytes=40 * 1024 * 1024),
        name="factor",
    )(pivot_rows, reduced, diagonal[None, :])
    return panels, new[0]


def pick_rows(wanted, row_ids, arrays):
    matches = wanted[:, None] == row_ids[None, :]
    slots = jnp.sum(
        jnp.where(matches, lax.broadcasted_iota(jnp.int32, matches.shape, 1), 0), axis=1
    )
    present = jnp.any(matches, axis=1)[:, None]
    return tuple((jnp.where(present, jnp.take(source, slots, axis=0), 0.0) for source in arrays))


def product(left, right):
    return jnp.dot(
        left, right.T, precision=lax.Precision.HIGHEST, preferred_element_type=jnp.float32
    )


def on_device(eri_cols, old_factor, residual_diag, pivots, row_ids):
    every_pivot = pivots.reshape(-1)
    old_rows, eri_rows = pick_rows(every_pivot, row_ids, (old_factor, eri_cols))
    old_rows, eri_rows = lax.psum((old_rows, eri_rows), "row")
    old_cross, old_gram = lax.psum(
        (product(old_factor, old_rows), product(old_rows, old_rows)), "col"
    )
    return factor(
        eri_rows - old_gram, eri_cols - old_cross, residual_diag, pivots.shape[0]
    )


def solution(mesh):
    placed = (P("row", None), P("row", "col"), P("row"), P(), P("row"))
    return jax.shard_map(
        on_device, mesh=mesh, in_specs=placed, out_specs=(P("row", None), P("row")), check_vma=False
    )
```

profile of v0, /device:TPU:0, one launch (start us, length us, event | category | flops | bytes accessed | tf_op | source)
XLA Modules:
  0.0 208.9 jit_solution(11960649120760344466)
XLA Ops:
  7.2 0.0 copy-start
  7.2 0.0 all-reduce.5.cloned.1.call-start
  7.2 0.0 copy-start.6
  7.2 0.0 copy-start.7
  7.2 1.0 compare_reduce_fusion
  8.3 0.0 copy-done.6
  8.3 0.0 copy-done.7
  8.3 0.2 fusion
  8.6 0.0 copy-done
  8.6 0.0 copy-start.2
  8.6 1.6 gather_fusion.1
  10.2 0.0 copy-done.2
  10.2 2.3 %gather_fusion = f32[512,512]{1,0:T(8,128)} fusion(f32[512,512]{1,0:T(8,128)S(1)} %copy-done.2, s32[1024]{0:T(1024)S(1)} %pad_clamp_fusion), kind=kCustom, calls=%fused_computation.clone | custom fusion | bytes 2099200 | tf_op jit(solution)/shard_map/jit(_take)/gather | solution.py:123
  12.6 2.8 %select_select_fusion = (f32[512,512]{1,0:T(8,128)}, f32[512,512]{1,0:T(8,128)}) fusion(f32[512,512]{1,0:T(8,128)S(1)} %gather_fusion.1, pred[512]{0:T(512)(128)(4,1)S(1)} %compare_and_fusion, pred[512]{0:T(512)(128)(4,1)S(1)} %compare_reduce_fusion, f32[512,512]{1,0:T(8,128)} %gather_fusion), kind=kLoop, calls=%fused_computation.6 | loop fusion | flops 1048576 | bytes 4195328 | tf_op jit(solution)/shard_map/jit(_where)/select_n | solution.py:123
  15.4 0.0 all-reduce.5.cloned.1.call-update
  15.4 0.0 all-reduce.7.cloned.1.call-start
  15.5 129.5 %all-reduce.5.cloned.1.call-done = (f32[512,512]{1,0:T(8,128)}, f32[512,512]{1,0:T(8,128)}) async-done(((f32[512,512]{1,0:T(8,128)}, f32[512,512]{1,0:T(8,128)}), (f32[512,512]{1,0:T(8,128)}, f32[512,512]{1,0:T(8,128)})) %all-reduce.5.cloned.1.call-update) | async-done | bytes 2097168 | tf_op jit(solution)/shard_map/psum | solution.py:135
  145.0 0.0 copy-start.3
  145.0 4.2 %convolution_bitcast_fusion = f32[512,512]{1,0:T(8,128)} fusion(f32[512,512]{1,0:T(8,128)} %get-tuple-element.8, f32[512,512]{1,0:T(8,128)S(1)} %copy-done), kind=kOutput, calls=%fused_computation.2 | convolution fusion | flops 1610612736 | bytes 3145728 | tf_op jit(solution)/shard_map/dot_general | solution.py:127
  149.1 0.0 copy-done.3
  149.1 2.8 %fusion.1 = f32[512,512]{1,0:T(8,128)} fusion(f32[512,512]{1,0:T(8,128)S(1)} %copy-done.3), kind=kOutput, calls=%fused_computation.11 | convolution fusion | flops 1610612736 | bytes 2097152 | tf_op jit(solution)/shard_map/dot_general | solution.py:127
  152.0 0.0 all-reduce.7.cloned.1.call-update
  152.0 20.8 %all-reduce.7.cloned.1.call-done = (f32[512,512]{1,0:T(8,128)}, f32[512,512]{1,0:T(8,128)}) async-done(((f32[512,512]{1,0:T(8,128)}, f32[512,512]{1,0:T(8,128)}), (f32[512,512]{1,0:T(8,128)}, f32[512,512]{1,0:T(8,128)})) %all-reduce.7.cloned.1.call-update) | async-done | bytes 2097168 | tf_op jit(solution)/shard_map/psum | solution.py:136
  172.8 0.0 copy-start.4
  172.8 0.0 copy-start.5
  172.8 1.6 sub.7.rows_ref
  174.4 0.0 copy-done.4
  174.4 0.3 copy-done.5
  174.6 0.0 copy-start.1
  174.6 0.2 sub.6.pivot_ref
  174.8 0.5 copy-done.1
  175.3 26.8 %factor.1 = (f32[512,512]{1,0:T(8,128)}, f32[1,512]{1,0:T(1,128)}) custom-call(f32[512,512]{1,0:T(8,128)S(1)} %sub.6.pivot_ref, f32[512,512]{1,0:T(8,128)S(1)} %sub.7.rows_ref, f32[1,512]{1,0:T(1,128)S(1)} %bitcast.9), custom_call_target="tpu_custom_call" | custom-call | tf_op jit(solution)/shard_map/factor/pallas_call | solution.py:102
  (3 shorter events, 0.0 us)
Async XLA Ops:
  7.2 1.4 copy-start
  7.2 137.8 %all-reduce.5.cloned.1.call-start = ((), (), s32[]{:S(2)}) async-start(), calls=%async_computation | async-start | bytes 4194304 | tf_op jit(solution)/shard_map/psum | solution.py:135
  7.2 1.0 copy-start.6
  7.2 1.0 copy-start.7
  8.6 1.6 copy-start.2
  15.4 157.3 %all-reduce.7.cloned.1.call-start = ((), (), s32[]{:S(2)}) async-start(), calls=%async_computation.1 | async-start | bytes 4194304 | tf_op jit(solution)/shard_map/psum | solution.py:136
  145.0 4.2 %copy-start.3 = (f32[512,512]{1,0:T(8,128)S(1)}, f32[512,512]{1,0:T(8,128)}, u32[]{:S(2)}) copy-start(f32[512,512]{1,0:T(8,128)} %get-tuple-element.8) | copy-start | bytes 3145732
  172.8 1.6 copy-start.4
  172.8 1.9 copy-start.5
  174.6 0.7 copy-start.1
Sparse Core Ops, SparseCore 0:
  15.6 129.3 all-reduce.4
  152.1 20.5 all-reduce.6
where the time goes:
time: 209 us
  waiting for transfers between devices  150 us (72%)
  Pallas kernels  26.8 us (13%)
  between operations  14.1 us (7%)
  matrix products  6.99 us (3%)
  other arithmetic  5.92 us (3%)
  local copies, waits for them, and re-layouts  4.71 us (2%)
    psum x1, waiting for transfers between devices, on_device(): old_rows, eri_rows = lax.psum((old_rows, eri_rows), 'row')  130 us
    pallas_call x1, Pallas kernels, factor(): pl.pallas_call(functools.partial(factor_kernel, steps), out_shape=(jax.Sh...  26.8 us
    psum x1, waiting for transfers between devices, on_device(): lax.psum((product(old_factor, old_rows), product(old_rows, old_rows)), 'c...  20.8 us
    dot_general x2, matrix products, product(): jnp.dot(left, right.T, precision=lax.Precision.HIGHEST, preferred_element...  6.99 us
  transfers between devices with their start and end apart: 2, of which 2 were waited for; matrix products, arithmetic and copies ran while one was open for 0% of the time, Pallas kernels for 0%

commit v1 on v0

v1 whole, which is shorter than its diff:
```python
import functools
import jax
import jax.numpy as jnp
from jax import lax
from jax.experimental import pallas as pl
from jax.experimental.pallas import tpu as pltpu
from jax.sharding import PartitionSpec as P

ROWS_T = (((1,), (1,)), ((), ()))
COLS_T = (((0,), (0,)), ((), ()))
SUB = 8
LANES = 128
MESH = pl.DeviceIdType.MESH
VMEM = pl.BlockSpec(memory_space=pltpu.VMEM)
SMEM = pl.BlockSpec(memory_space=pltpu.SMEM)
F32 = jnp.float32
BF16 = jnp.bfloat16


def split(x):
    hi = x.astype(BF16)
    return hi, (x - hi.astype(F32)).astype(BF16)


def dot_t(a, b):
    f = functools.partial(
        lax.dot_general, dimension_numbers=ROWS_T, preferred_element_type=F32
    )
    return f(a[0], b[0]) + (f(a[0], b[1]) + f(a[1], b[0]))


def inverse_factor(a):
    n = a.shape[0]
    groups = n // SUB
    row = lax.broadcasted_iota(jnp.int32, (SUB, n), 0)
    lane = lax.broadcasted_iota(jnp.int32, (SUB, n), 1)
    A = [a[SUB * i : SUB * i + SUB, :] for i in range(groups)]
    W = [jnp.where(lane == row + SUB * i, 1.0, 0.0) for i in range(groups)]
    out = []
    wide = lambda v: jnp.broadcast_to(v, (SUB, n))
    for g in range(groups):
        j = SUB * g
        C = [[wide(A[i][:, j + k : j + k + 1]) for k in range(SUB)] for i in range(g, groups)]
        D = [[wide(C[0][l][k : k + 1, :]) for l in range(k + 1)] for k in range(SUB)]
        r = [wide(A[g][k : k + 1, :]) for k in range(SUB)]
        w = [wide(W[g][k : k + 1, :]) for k in range(SUB)]
        inv, m = [], [[None] * SUB for _ in range(SUB)]
        done = jnp.zeros((SUB, n), F32)
        for k in range(SUB):
            root = lax.rsqrt(D[k][k])
            inv.append(root * root)
            done = jnp.where(row == k, w[k] * root, done)
            for i in range(k + 1, SUB):
                m[i][k] = D[i][k] * inv[k]
            for i in range(k + 1, SUB):
                for l in range(k + 1, i + 1):
                    D[i][l] = D[i][l] - m[i][k] * D[l][k]
                r[i] = r[i] - m[i][k] * r[k]
                w[i] = w[i] - m[i][k] * w[k]
        out.append(done)
        if g + 1 == groups:
            break
        s, t = [None] * SUB, [None] * SUB
        for k in reversed(range(SUB)):
            s[k], t[k] = r[k] * inv[k], w[k] * inv[k]
            for i in reversed(range(k + 1, SUB)):
                s[k] = s[k] - m[i][k] * s[i]
                t[k] = t[k] - m[i][k] * t[i]
        for i in range(g + 1, groups):
            c = C[i - g]
            for k in range(SUB):
                A[i] = A[i] - c[k] * s[k]
                W[i] = W[i] - c[k] * t[k]
    return jnp.concatenate(out, axis=0)


def pack_kernel(cap, window_ref, pivot_ref, ids_ref, old_ref, eri_ref, out_ref):
    steps, width = pivot_ref.shape
    slots = out_ref.shape[1]
    part = out_ref.shape[2]
    groups = ids_ref.shape[0]
    half = eri_ref.shape[1] // 2
    ids = ids_ref[...]

    def find(j, at):
        return jnp.where(ids == pivot_ref[j // width, j % width], j + 1, at)

    at = lax.fori_loop(0, steps * width, find, jnp.zeros_like(ids), unroll=16)
    owned = jnp.where(at > 0, 1.0, 0.0)
    below = lax.broadcasted_iota(jnp.int32, (LANES, LANES), 0)
    right = lax.broadcasted_iota(jnp.int32, (LANES, LANES), 1)
    ahead = jnp.where(below < right, 1.0, 0.0).astype(BF16)
    rank = lax.dot_general(
        owned.astype(BF16), ahead, (((1,), (0,)), ((), ())), preferred_element_type=F32
    )
    first = window_ref[0] * cap
    slot = lax.broadcasted_iota(jnp.int32, (slots, LANES), 0)
    passed = jnp.zeros((1, 1), F32)
    picks, numbers = [], []
    for g in range(groups):
        here = (rank[g : g + 1] + passed).astype(jnp.int32) - first
        passed = passed + jnp.sum(owned[g : g + 1], axis=1, keepdims=True)
        here = jnp.where((owned[g : g + 1] > 0) & (here >= 0) & (here < cap), here, -1)
        picks.append(jnp.where(slot == here, 1.0, 0.0))
        numbers.append(at[g : g + 1])
    pick = jnp.concatenate(picks, axis=1).astype(BF16)
    number = jnp.concatenate(numbers, axis=1)
    pair = jnp.concatenate([number // 16, number % 16] + [jnp.zeros_like(number)] * 6, axis=0)
    pair = pair.astype(F32).astype(BF16)
    lines = lax.dot_general(pair, pick, ROWS_T, preferred_element_type=F32)
    line = lines[0:1] * 16.0 + lines[1:2]
    lane = lax.broadcasted_iota(jnp.int32, (1, LANES), 1)
    line = jnp.concatenate([line, jnp.zeros((1, LANES - slots), F32)], axis=1)
    line = jnp.where(lane == LANES - 1, passed, line)

    def take(x):
        f = functools.partial(
            lax.dot_general,
            dimension_numbers=(((1,), (0,)), ((), ())),
            preferred_element_type=F32,
        )
        hi, lo = split(x)
        return f(pick, hi) + f(pick, lo)

    core = lax.axis_index("col")
    out_ref[0] = take(old_ref[:, :part])
    out_ref[0, slots - 1 : slots, :LANES] = line
    rest = old_ref.shape[1] - part
    out_ref[1, :, :rest] = take(old_ref[:, part:])
    out_ref[1, :, rest:] = take(eri_ref[:, pl.ds(pl.multiple_of(core * half, LANES), half)])


def pack(window, pivots, ids, old, eri, slots):
    width = (old.shape[1] + eri.shape[1] // 2) // 2
    return pl.pallas_call(
        functools.partial(pack_kernel, slots - 1),
        out_shape=jax.ShapeDtypeStruct((2, slots, width), F32),
        in_specs=[SMEM, SMEM, VMEM, VMEM, VMEM],
        out_specs=VMEM,
        name="pack",
    )(window, pivots, ids, old, eri)


def spread_kernel(grid, mine_ref, old_ref, all_ref, other_ref, *sems):
    deep, high, wide = grid
    fine = deep * high * wide <= 16
    own_sem, first_send, near_send, far_send, core_send = sems[:5]
    first_recv, recv, core_recv, old_sems = sems[5:]
    me = lax.axis_index("row")
    core = lax.axis_index("col")
    z, y, x = me // (high * wide), me // wide % high, me % wide
    chip = lambda z, y, x: (z * high + y) * wide + x
    steps = lambda at, size: [lax.rem(at + o, size) for o in range(1, size)]
    partner = (me, 1 - core)

    barrier = pltpu.get_barrier_semaphore()
    greet = [(chip(o, y, x), core) for o in steps(z, deep)]
    greet += [(chip(z, o, x), core) for o in steps(y, high)]
    greet += [(chip(z, y, o), core) for o in steps(x, wide)]
    greet.append(partner)
    for device in greet:
        pl.semaphore_signal(barrier, inc=1, device_id=device, device_id_type=MESH)
    pl.semaphore_wait(barrier, len(greet))

    flying = []

    def send(src, dst, send_sem, recv_sem, device):
        copy = pltpu.make_async_remote_copy(
            src_ref=src, dst_ref=dst, send_sem=send_sem, recv_sem=recv_sem,
            device_id=device, device_id_type=MESH,
        )
        copy.start()
        flying.append(copy)

    def await_block(ref, sem):
        pltpu.make_async_remote_copy(
            src_ref=ref, dst_ref=ref, send_sem=sem, recv_sem=sem,
            device_id=partner, device_id_type=MESH,
        ).wait_recv()

    def block(colour, zs, y, x):
        return all_ref.at[core, colour, zs, y, x]

    own = [
        pltpu.make_async_copy(mine_ref.at[k], all_ref.at[core, k, z, y, x], own_sem.at[k])
        for k in range(2)
    ]
    for k in range(2):
        own[k].start()
    for k in range(2):
        for i, o in enumerate(steps(z, deep)):
            send(mine_ref.at[k], block(k, z, y, x), first_send.at[k, i], first_recv.at[k, z], (chip(o, y, x), core))

    chunks = [z] + steps(z, deep) if fine else [None]
    near = lambda k: [(y, o) for o in steps(x, wide)] if k == 0 else [(o, x) for o in steps(y, high)]
    far = lambda k: [(o, x) for o in steps(y, high)] if k == 0 else [(y, o) for o in steps(x, wide)]

    def to_core(k, q, i, zs, y, x):
        ref = block(k, zs, y, x)
        send(ref, ref, core_send.at[k, q, i], core_recv.at[k, chunk_at(zs), y, x], partner)

    def chunk_at(zs):
        return zs if fine else 0

    def rows(zs):
        return zs if fine else slice(None)

    for q, at in enumerate(chunks):
        zs = rows(at)
        mine = fine and q == 0
        for k in range(2):
            if q == 0:
                if not fine:
                    for o in steps(z, deep):
                        await_block(block(k, o, y, x), first_recv.at[k, o])
                    own[k].wait()
            else:
                await_block(block(k, zs, y, x), first_recv.at[k, zs])
            src = mine_ref.at[k] if mine else block(k, zs, y, x)
            sem = recv.at[k, chunk_at(zs), y, x]
            for i, (b, c) in enumerate(near(k)):
                send(src, block(k, zs, y, x), near_send.at[k, q, i], sem, (chip(z, b, c), core))
            for i, (b, c) in enumerate(far(k)):
                send(src, block(k, zs, y, x), far_send.at[k, q, 0, i], sem, (chip(z, b, c), core))
            send(src, block(k, zs, y, x), core_send.at[k, q, 0], core_recv.at[k, chunk_at(zs), y, x], partner)
    old_copy = pltpu.make_async_remote_copy(
        src_ref=old_ref, dst_ref=other_ref, send_sem=old_sems.at[0], recv_sem=old_sems.at[1],
        device_id=partner, device_id_type=MESH,
    )
    old_copy.start()
    flying.append(old_copy)
    for q, at in enumerate(chunks):
        zs = rows(at)
        for k in range(2):
            for n, (b, c) in enumerate(near(k)):
                ref = block(k, zs, b, c)
                await_block(ref, recv.at[k, chunk_at(zs), b, c])
                for i, (fb, fc) in enumerate(far(k)):
                    send(ref, ref, far_send.at[k, q, 1 + n, i], recv.at[k, chunk_at(zs), b, c], (chip(z, fb, fc), core))
                to_core(k, q, 1 + n, zs, b, c)
    for q, at in enumerate(chunks):
        zs = rows(at)
        for k in range(2):
            index = 1 + len(near(k))
            for fb, fc in far(k):
                for b, c in [(y, x)] + near(k):
                    there = (fb, c) if k == 0 else (b, fc)
                    ref = block(k, zs, *there)
                    await_block(ref, recv.at[k, chunk_at(zs), *there])
                    to_core(k, q, index, zs, *there)
                    index += 1
    if fine:
        for k in range(2):
            own[k].wait()
    for q, at in enumerate(chunks):
        zs = rows(at)
        for k in range(2):
            for b in range(high):
                for c in range(wide):
                    ref = all_ref.at[1 - core, k, zs, b, c]
                    await_block(ref, core_recv.at[k, chunk_at(zs), b, c])
    old_copy.wait_recv()
    for copy in flying:
        copy.wait_send()


def spread(grid, mine, old):
    deep, high, wide = grid
    _, slots, width = mine.shape
    chunks = deep if deep * high * wide <= 16 else 1
    cells = high * wide
    peers = max(high, wide)
    sem = pltpu.SemaphoreType.DMA
    return pl.pallas_call(
        functools.partial(spread_kernel, grid),
        out_shape=(
            jax.ShapeDtypeStruct((2, 2, deep, high, wide, slots, width), F32),
            jax.ShapeDtypeStruct(old.shape, F32),
        ),
        in_specs=[pl.BlockSpec(memory_space=pl.ANY)] * 2,
        out_specs=(VMEM, pl.BlockSpec(memory_space=pl.ANY)),
        scratch_shapes=[
            sem((2,)),
            sem((2, max(deep - 1, 1))),
            sem((2, chunks, max(peers - 1, 1))),
            sem((2, chunks, peers, max(peers - 1, 1))),
            sem((2, chunks, cells)),
            sem((2, deep)),
            sem((2, chunks, high, wide)),
            sem((2, chunks, high, wide)),
            sem((2,)),
        ],
        compiler_params=pltpu.CompilerParams(
            collective_id=0, has_side_effects=True, vmem_limit_bytes=48 * 1024 * 1024
        ),
        name="spread",
    )(mine, old)


def finish_kernel(
    steps, chips, all_ref, own_ref, other_ref, eri_ref, diag_ref, panel_ref, new_ref,
    work, old_hi, old_lo,
):
    rows, piv = eri_ref.shape
    width = piv // steps
    part = all_ref.shape[3]
    slots = all_ref.shape[2] // chips
    half = own_ref.shape[1]
    core = lax.axis_index("col")
    f = functools.partial(lax.dot_general, preferred_element_type=F32)

    line = [all_ref[0, 0, slots * i + slots - 1 : slots * (i + 1), :LANES] for i in range(chips)]
    if chips < LANES:
        line.append(jnp.zeros((LANES - chips, LANES), F32))
    line = jnp.concatenate(line, axis=0)
    held = jnp.transpose(line)
    number = lax.broadcasted_iota(jnp.int32, (slots, piv), 1).astype(F32) + 1.0
    place = jnp.concatenate(
        [
            jnp.where(jnp.broadcast_to(held[:slots, i : i + 1], (slots, piv)) == number, 1.0, 0.0)
            for i in range(chips)
        ],
        axis=0,
    ).astype(BF16)
    for c in range(2):
        for k in range(2):
            hi, lo = split(all_ref[c, k])
            hi = f(place, hi, COLS_T)
            lo = f(place, lo, COLS_T)
            if k == 0:
                old_hi[c, :, :part] = hi.astype(BF16)
                old_lo[c, :, :part] = lo.astype(BF16)
            else:
                rest = half - part
                old_hi[c, :, part:] = hi[:, :rest].astype(BF16)
                old_lo[c, :, part:] = lo[:, :rest].astype(BF16)
                eri = piv // 2
                work[:piv, c * eri : (c + 1) * eri] = hi[:, rest:] + lo[:, rest:]
    both = [(old_hi[c], old_lo[c]) for c in range(2)]
    work[:piv, :] = work[:piv, :] - (dot_t(both[0], both[0]) + dot_t(both[1], both[1]))
    mine = (old_hi[core], old_lo[core])
    theirs = (old_hi[1 - core], old_lo[1 - core])
    work[piv:, :] = eri_ref[...] - (
        dot_t(split(own_ref[...]), mine) + dot_t(split(other_ref[...]), theirs)
    )
    new_ref[...] = diag_ref[...]
    ones = jnp.ones((SUB, width), BF16)

    def step(s, carry):
        at = pl.ds(pl.multiple_of(s * width, width), width)
        inv = split(inverse_factor(work[at, at]))
        solved = dot_t(split(work[:, at]), inv)
        own = solved[piv:]
        panel_ref[:, at] = own
        hi, lo = split(own * own)
        new_ref[...] -= (f(ones, hi, ROWS_T) + f(ones, lo, ROWS_T))[:1]

        @pl.when(s < steps - 1)
        def _():
            both = split(solved)
            work[...] -= dot_t(both, (both[0][:piv], both[1][:piv]))

        return carry

    lax.fori_loop(0, steps, step, 0)


def finish(steps, chips, everything, own, other, eri, diagonal):
    rows, piv = eri.shape
    panels, new = pl.pallas_call(
        functools.partial(finish_kernel, steps, chips),
        out_shape=(
            jax.ShapeDtypeStruct((rows, piv), F32),
            jax.ShapeDtypeStruct((1, rows), F32),
        ),
        in_specs=[VMEM] * 5,
        out_specs=[VMEM] * 2,
        scratch_shapes=[
            pltpu.VMEM((piv + rows, piv), F32),
            pltpu.VMEM((2, piv, own.shape[1]), BF16),
            pltpu.VMEM((2, piv, own.shape[1]), BF16),
        ],
        compiler_params=pltpu.CompilerParams(vmem_limit_bytes=56 * 1024 * 1024),
        name="finish",
    )(everything, own, other, eri, diagonal[None, :])
    return panels, new[0]


def torus(chips):
    side = 1
    while 2 * (side + 1) ** 3 <= chips:
        side += 1
    return (2 * side, side, side) if 2 * side**3 == chips else (chips, 1, 1)


def slots_for(pivots, chips):
    mean = -(-pivots // chips)
    return min(LANES - 8, -(-(mean + max(12, mean // 2)) // 16) * 16)


def on_device(grid, eri_cols, old_factor, residual_diag, pivots, row_ids):
    steps, width = pivots.shape
    piv = steps * width
    chips = grid[0] * grid[1] * grid[2]
    slots = slots_for(piv, chips)
    cap = slots - 1
    ids = row_ids.reshape(-1, LANES)

    def gather(window):
        mine = pack(jnp.full((1,), window, jnp.int32), pivots, ids, old_factor, eri_cols, slots)
        everything, other = spread(grid, mine, old_factor)
        return everything.reshape(2, 2, chips * slots, -1), other

    def line_of(everything):
        return everything[0, 0].reshape(chips, slots, -1)[:, slots - 1, :LANES]

    everything, other = gather(0)
    most = jnp.max(line_of(everything)[:, LANES - 1]).astype(jnp.int32)
    windows = (most + cap - 1) // cap

    def placed(everything):
        number = line_of(everything)[:, :slots].reshape(-1)
        one = lax.broadcasted_iota(jnp.int32, (piv, chips * slots), 0) + 1 == number[None, :].astype(jnp.int32)
        filled = jnp.arange(chips * slots) % slots < cap
        dot = functools.partial(jnp.einsum, "ps,abse->abpe", precision=lax.Precision.HIGHEST)
        return dot(jnp.where(one & filled[None, :], 1.0, 0.0), everything)

    def more(state):
        _, everything = state
        rows = lax.fori_loop(
            1, windows, lambda w, rows: rows + placed(gather(w)[0]), placed(everything)
        )
        rows = jnp.pad(rows, ((0, 0), (0, 0), (0, chips * cap - piv), (0, 0)))
        rows = rows.reshape(2, 2, chips, cap, -1)
        number = jnp.arange(chips * cap) + 1
        number = jnp.where(number <= piv, number, 0).reshape(chips, cap).astype(F32)
        line = jnp.pad(number, ((0, 0), (0, rows.shape[-1] - cap)))
        line = jnp.broadcast_to(line[None, None, :, None], (2, 2, chips, 1, rows.shape[-1]))
        rows = jnp.concatenate([rows, line], axis=3)
        return jnp.bool_(False), rows.reshape(everything.shape)

    _, everything = lax.while_loop(lambda s: s[0], more, (windows > 1, everything))
    return finish(steps, chips, everything, old_factor, other, eri_cols, residual_diag)


def solution(mesh):
    grid = torus(mesh.shape["row"])
    placed = (P("row", None), P("row", "col"), P("row"), P(), P("row"))
    return jax.shard_map(
        functools.partial(on_device, grid),
        mesh=mesh, in_specs=placed, out_specs=(P("row", None), P("row")), check_vma=False,
    )
```

time: 209 us -> 85.6 us (0.41)
  the two profiles are of different devices: /device:TPU:0 before, /device:TPU:11 now
where the time goes in v1:
time: 85.6 us; the launch traced here: 85.5 us
  Pallas kernels  79.1 us (92%)
  local copies, waits for them, and re-layouts  4.13 us (5%)
  between operations  1.38 us (2%)
    pallas_call x1, Pallas kernels, finish(): pl.pallas_call(functools.partial(finish_kernel, steps, chips), out_shape=...  36.8 us
    pallas_call x1, Pallas kernels, spread(): pl.pallas_call(functools.partial(spread_kernel, grid), out_shape=(jax.Sha...  35.6 us
    pallas_call x1, Pallas kernels, pack(): pl.pallas_call(functools.partial(pack_kernel, slots - 1), out_shape=jax.S...  6.77 us
    unnamed x10, local copies, waits for them, and re-layouts  4.04 us

profile of v1, /device:TPU:11, one launch (start us, length us, event | category | flops | bytes accessed | tf_op | source)
XLA Modules:
  0.0 85.5 jit_solution(8930264936300415434)
XLA Ops:
  0.6 0.0 copy-start.6
  0.6 0.0 copy-start.5
  0.6 6.8 %pack.2.mine_ref = f32[2,48,384]{2,1,0:T(8,128)} custom-call(s32[1]{0:T(128)} %constant.79.clone.1.window_ref, s32[4,128]{1,0:T(4,128)} %pivot_ref.1, s32[4,128]{1,0:T(4,128)} %bitcast.53, f32[512,512]{1,0:T(8,128)} %own_ref.1, f32[512,512]{1,0:T(8,128)} %eri_ref.3), custom_call_target="tpu_custom_call" | custom-call | tf_op jit(solution)/shard_map/pack/pallas_call | solution.py:135
  7.4 0.0 copy-start.3
  7.4 0.9 %copy-done.3 = f32[2,48,384]{2,1,0:T(8,128)S(1)} copy-done((f32[2,48,384]{2,1,0:T(8,128)S(1)}, f32[2,48,384]{2,1,0:T(8,128)}, u32[]{:S(2)}) %copy-start.3) | copy-done | bytes 147480
  8.3 35.6 %spread.5 = (f32[2,2,4,2,2,48,384]{6,5,4,3,2,1,0:T(8,128)S(1)}, f32[512,512]{1,0:T(8,128)S(1)}) custom-call(f32[2,48,384]{2,1,0:T(8,128)S(1)} %copy-done.3, f32[512,512]{1,0:T(8,128)} %own_ref.1), custom_call_target="tpu_custom_call" | custom-call | tf_op jit(solution)/shard_map/spread/pallas_call | solution.py:274
  43.9 0.0 copy-start.2
  43.9 0.9 %copy-done.2 = f32[512,512]{1,0:T(8,128)} copy-done((f32[512,512]{1,0:T(8,128)}, f32[512,512]{1,0:T(8,128)S(1)}, u32[]{:S(2)}) %copy-start.2) | copy-done | bytes 1048600
  44.9 0.0 copy-start.4
  44.9 2.2 %copy-done.4 = f32[2,2,4,2,2,48,384]{6,5,4,3,2,1,0:T(8,128)} copy-done((f32[2,2,4,2,2,48,384]{6,5,4,3,2,1,0:T(8,128)}, f32[2,2,4,2,2,48,384]{6,5,4,3,2,1,0:T(8,128)S(1)}, u32[]{:S(2)}) %copy-start.4) | copy-done | bytes 4718616
  47.0 0.1 slice.44
  47.1 0.7 slice_reduce_fusion
  48.5 0.0 copy-done.6
  48.5 0.0 copy-done.5
  48.5 0.2 while.20
  48.7 36.8 %finish.1 = (f32[512,512]{1,0:T(8,128)}, f32[1,512]{1,0:T(1,128)}) custom-call(f32[2,2,768,384]{3,2,1,0:T(8,128)} %get-tuple-element.298, f32[512,512]{1,0:T(8,128)} %get-tuple-element.302, f32[512,512]{1,0:T(8,128)} %copy-done.2, f32[512,512]{1,0:T(8,128)} %get-tuple-element.303, f32[1,512]{1,0:T(1,128)} %bitcast.58), custom_call_target="tpu_custom_call" | custom-call | tf_op jit(solution)/shard_map/finish/pallas_call | solution.py:370
  (1 shorter events, 0.0 us)
Async XLA Ops:
  0.6 47.8 %copy-start.6 = (s32[512]{0:T(512)S(1)}, s32[512]{0:T(512)}, u32[]{:S(2)}) copy-start(s32[512]{0:T(512)} %param.13) | copy-start | bytes 6148
  0.6 47.8 %copy-start.5 = (s32[4,128]{1,0:T(4,128)S(1)}, s32[4,128]{1,0:T(4,128)}, u32[]{:S(2)}) copy-start(s32[4,128]{1,0:T(4,128)} %pivot_ref.1) | copy-start | bytes 6148
  7.4 0.9 %copy-start.3 = (f32[2,48,384]{2,1,0:T(8,128)S(1)}, f32[2,48,384]{2,1,0:T(8,128)}, u32[]{:S(2)}) copy-start(f32[2,48,384]{2,1,0:T(8,128)} %pack.2.mine_ref) | copy-start | bytes 442372
  43.9 1.0 %copy-start.2 = (f32[512,512]{1,0:T(8,128)}, f32[512,512]{1,0:T(8,128)S(1)}, u32[]{:S(2)}) copy-start(f32[512,512]{1,0:T(8,128)S(1)} %get-tuple-element.134.other_ref) | copy-start | bytes 3145732
  44.9 2.2 %copy-start.4 = (f32[2,2,4,2,2,48,384]{6,5,4,3,2,1,0:T(8,128)}, f32[2,2,4,2,2,48,384]{6,5,4,3,2,1,0:T(8,128)S(1)}, u32[]{:S(2)}) copy-start(f32[2,2,4,2,2,48,384]{6,5,4,3,2,1,0:T(8,128)S(1)} %get-tuple-element.132) | copy-start | bytes 14155780

commit v2 on v1

--- a/solution.py
+++ b/solution.py
@@ -34,43 +34,56 @@
     groups = n // SUB
     row = lax.broadcasted_iota(jnp.int32, (SUB, n), 0)
     lane = lax.broadcasted_iota(jnp.int32, (SUB, n), 1)
-    A = [a[SUB * i : SUB * i + SUB, :] for i in range(groups)]
-    W = [jnp.where(lane == row + SUB * i, 1.0, 0.0) for i in range(groups)]
+    M = [a[SUB * i : SUB * i + SUB, :] for i in range(groups)]
+    over = lambda v, k: jnp.broadcast_to(v[k : k + 1, :], (SUB, n))
+    columns = lambda v, j: [jnp.broadcast_to(v[:, j + k : j + k + 1], (SUB, n)) for k in range(SUB)]
     out = []
-    wide = lambda v: jnp.broadcast_to(v, (SUB, n))
+    V = columns(M[0], 0)
     for g in range(groups):
         j = SUB * g
-        C = [[wide(A[i][:, j + k : j + k + 1]) for k in range(SUB)] for i in range(g, groups)]
-        D = [[wide(C[0][l][k : k + 1, :]) for l in range(k + 1)] for k in range(SUB)]
-        r = [wide(A[g][k : k + 1, :]) for k in range(SUB)]
-        w = [wide(W[g][k : k + 1, :]) for k in range(SUB)]
-        inv, m = [], [[None] * SUB for _ in range(SUB)]
-        done = jnp.zeros((SUB, n), F32)
+        ahead = g + 1 < groups
+        if ahead:
+            U = columns(M[g + 1], j)
+            N = columns(M[g + 1], j + SUB)
+        here = (lane >= j) & (lane < j + SUB)
+        M[g] = jnp.where(here, jnp.where(lane == row + j, 1.0, 0.0), M[g])
+        if ahead:
+            M[g + 1] = jnp.where(here, 0.0, M[g + 1])
+        roots = jnp.zeros((SUB, n), F32)
+        invs = jnp.zeros((SUB, n), F32)
         for k in range(SUB):
-            root = lax.rsqrt(D[k][k])
-            inv.append(root * root)
-            done = jnp.where(row == k, w[k] * root, done)
-            for i in range(k + 1, SUB):
-                m[i][k] = D[i][k] * inv[k]
-            for i in range(k + 1, SUB):
-                for l in range(k + 1, i + 1):
-                    D[i][l] = D[i][l] - m[i][k] * D[l][k]
-                r[i] = r[i] - m[i][k] * r[k]
-                w[i] = w[i] - m[i][k] * w[k]
-        out.append(done)
-        if g + 1 == groups:
+            root = lax.rsqrt(over(V[k], k))
+            inv = root * root
+            roots = jnp.where(row == k, root, roots)
+            invs = jnp.where(row == k, inv, invs)
+            down = jnp.where(row > k, V[k], 0.0)
+            top = [None] * SUB
+            for l in range(k + 1, SUB):
+                top[l] = over(V[k], l)
+                V[l] = V[l] - (down * top[l]) * inv
+            r = over(M[g], k)
+            M[g] = M[g] - (down * inv) * r
+            if ahead:
+                u = U[k] * inv
+                for l in range(k + 1, SUB):
+                    U[l] = U[l] - u * top[l]
+                M[g + 1] = M[g + 1] - u * r
+                for l in range(SUB):
+                    N[l] = N[l] - u * over(U[k], l)
+        out.append(jnp.where(lane < j + SUB, M[g] * roots, 0.0))
+        if not ahead:
             break
-        s, t = [None] * SUB, [None] * SUB
-        for k in reversed(range(SUB)):
-            s[k], t[k] = r[k] * inv[k], w[k] * inv[k]
-            for i in reversed(range(k + 1, SUB)):
-                s[k] = s[k] - m[i][k] * s[i]
-                t[k] = t[k] - m[i][k] * t[i]
-        for i in range(g + 1, groups):
-            c = C[i - g]
-            for k in range(SUB):
-                A[i] = A[i] - c[k] * s[k]
-                W[i] = W[i] - c[k] * t[k]
+        if g + 2 < groups:
+            S = M[g] * invs
+            for i in reversed(range(1, SUB)):
+                S = S - (jnp.where(row < i, V[i], 0.0) * invs) * over(S, i)
+            S = [over(S, k) for k in range(SUB)]
+            for i in range(g + 2, groups):
+                C = columns(M[i], j)
+                M[i] = jnp.where(here, 0.0, M[i])
+                for k in range(SUB):
+                    M[i] = M[i] - C[k] * S[k]
+        V = N
     return jnp.concatenate(out, axis=0)
 
 
@@ -109,9 +122,7 @@
     pair = pair.astype(F32).astype(BF16)
     lines = lax.dot_general(pair, pick, ROWS_T, preferred_element_type=F32)
     line = lines[0:1] * 16.0 + lines[1:2]
-    lane = lax.broadcasted_iota(jnp.int32, (1, LANES), 1)
     line = jnp.concatenate([line, jnp.zeros((1, LANES - slots), F32)], axis=1)
-    line = jnp.where(lane == LANES - 1, passed, line)
 
     def take(x):
         f = functools.partial(
@@ -297,78 +308,520 @@
     )(mine, old)
 
 
+def gather_kernel(
+    grid, pivot_ref, ids_ref, old_hbm, eri_hbm,
+    gram_ref, hi_ref, lo_ref, old_hi_ref, old_lo_ref, most_ref,
+    old, other, eri, mine, every,
+    in_sems, own_sem, z_send, near_send, far_send, core_send, recv, core_recv, old_sems,
+):
+    deep, high, wide = grid
+    cells = high * wide
+    slots, width = mine.shape
+    cap = slots - 1
+    part = width // 2
+    half = old.shape[1]
+    piv = gram_ref.shape[0]
+    groups = ids_ref.shape[0]
+    pages = pivot_ref.shape[0]
+    me = lax.axis_index("row")
+    core = lax.axis_index("col")
+    z, y, x = me // cells, me // wide % high, me % wide
+    partner = (me, 1 - core)
+    chip = lambda z, y, x: ((z * high + y) * wide + x, core)
+    around = lambda at, size: [lax.rem(at + o, size) for o in range(1, size)]
+
+    barrier = pltpu.get_barrier_semaphore()
+    signal = functools.partial(pl.semaphore_signal, barrier, inc=1, device_id_type=MESH)
+    beside = [chip(z, o, x) for o in around(y, high)] + [chip(z, y, o) for o in around(x, wide)]
+    for device in beside + [partner]:
+        signal(device_id=device)
+
+    @pl.when(z > 0)
+    def _():
+        signal(device_id=chip(z - 1, y, x))
+
+    @pl.when(z < deep - 1)
+    def _():
+        signal(device_id=chip(z + 1, y, x))
+
+    loads = [
+        pltpu.make_async_copy(old_hbm, old, in_sems.at[0]),
+        pltpu.make_async_copy(eri_hbm, eri, in_sems.at[1]),
+    ]
+    for load in loads:
+        load.start()
+
+    dot = functools.partial(
+        lax.dot_general, dimension_numbers=(((1,), (0,)), ((), ())), preferred_element_type=F32
+    )
+    wanted = [
+        jnp.transpose(jnp.broadcast_to(pivot_ref[b : b + 1].astype(F32), (LANES, LANES)))
+        for b in range(pages)
+    ]
+    count = lax.broadcasted_iota(jnp.int32, (LANES, LANES), 0).astype(F32) + 1.0
+    at = []
+    for g in range(groups):
+        ids = jnp.broadcast_to(ids_ref[g : g + 1].astype(F32), (LANES, LANES))
+        found = [jnp.where(wanted[b] == ids, count + float(LANES * b), 0.0) for b in range(pages)]
+        at.append(jnp.sum(functools.reduce(jnp.add, found), axis=0, keepdims=True))
+    owned = [jnp.where(v > 0, 1.0, 0.0) for v in at]
+    below = lax.broadcasted_iota(jnp.int32, (LANES, LANES), 0)
+    right = lax.broadcasted_iota(jnp.int32, (LANES, LANES), 1)
+    ahead = jnp.where(below < right, 1.0, 0.0).astype(BF16)
+    rank = dot(jnp.concatenate(owned + [jnp.zeros((-groups % 8, LANES), F32)], axis=0).astype(BF16), ahead)
+    passed = jnp.zeros((1, 1), F32)
+    heres = []
+    for g in range(groups):
+        here = rank[g : g + 1] + passed
+        passed = passed + jnp.sum(owned[g], axis=1, keepdims=True)
+        heres.append(jnp.where((owned[g] > 0) & (here < cap), here, -1.0 - slots * cells))
+    here = jnp.concatenate(heres, axis=1)
+    number = jnp.concatenate(at, axis=1)
+    rows = here.shape[1]
+    slot = lax.broadcasted_iota(jnp.int32, (slots, rows), 0).astype(F32)
+    pick = jnp.where(slot == here, 1.0, 0.0).astype(BF16)
+    place = lax.broadcasted_iota(jnp.int32, (slots * cells, rows), 0)
+    first = (lax.rem(me, cells) * slots).astype(F32)
+    seat = jnp.where(place.astype(F32) == here + first, 1.0, 0.0).astype(BF16)
+    high_part = jnp.floor(number * (1.0 / 16.0))
+    pair = jnp.concatenate([high_part, number - 16.0 * high_part, jnp.zeros((6, rows), F32)], axis=0)
+    lines = lax.dot_general(pair.astype(BF16), seat, ROWS_T, preferred_element_type=F32)
+    line = lines[0:1] * 16.0 + lines[1:2]
+    line = jnp.concatenate([line, jnp.broadcast_to(passed, (1, part - slots * cells))], axis=1)
+
+    def take(v):
+        hi, lo = split(v)
+        return dot(pick, hi) + dot(pick, lo)
+
+    loads[0].wait()
+    mine[:, :half] = take(old[...])
+    mine[slots - 1 : slots, :part] = line
+    loads[1].wait()
+    mine[:, half:] = take(eri[:, pl.ds(pl.multiple_of(core * (piv // 2), LANES), piv // 2)])
+
+    ends = (z + deep - 1) // deep + (2 * deep - 2 - z) // deep
+    pl.semaphore_wait(barrier, len(beside) + 1 + ends)
+
+    colour = [slice(0, part), slice(part, width)]
+
+    def block(k, zz, b, c):
+        return every.at[core, zz, b, c, :, colour[k]]
+
+    def remote(src, dst, send_sem, recv_sem, device):
+        return pltpu.make_async_remote_copy(
+            src_ref=src, dst_ref=dst, send_sem=send_sem, recv_sem=recv_sem,
+            device_id=device, device_id_type=MESH,
+        )
+
+    def await_block(ref, sem):
+        remote(ref, ref, sem, sem, partner).wait_recv()
+
+    near = [[(y, o) for o in around(x, wide)], [(o, x) for o in around(y, high)]]
+    far = [near[1], near[0]]
+
+    def upward(k, zz, src):
+        return remote(src, block(k, zz, y, x), z_send.at[k, 0, zz], recv.at[k, zz, y, x], chip(z + 1, y, x))
+
+    def downward(k, zz, src):
+        return remote(src, block(k, zz, y, x), z_send.at[k, 1, zz], recv.at[k, zz, y, x], chip(z - 1, y, x))
+
+    def line_sends(k, zz, src):
+        out = []
+        for i, (b, c) in enumerate(near[k]):
+            out.append(remote(src, block(k, zz, y, x), near_send.at[k, zz, i], recv.at[k, zz, y, x], chip(z, b, c)))
+        for i, (b, c) in enumerate(far[k]):
+            out.append(remote(src, block(k, zz, y, x), far_send.at[k, zz, 0, i], recv.at[k, zz, y, x], chip(z, b, c)))
+        return out
+
+    def onward(k, zz, n, b, c):
+        ref = block(k, zz, b, c)
+        return [
+            remote(ref, ref, far_send.at[k, zz, 1 + n, i], recv.at[k, zz, b, c], chip(z, fb, fc))
+            for i, (fb, fc) in enumerate(far[k])
+        ]
+
+    def across(zz, b, c, src=None):
+        ref = every.at[core, zz, b, c]
+        return remote(ref if src is None else src, ref, core_send.at[zz, b, c], core_recv.at[zz, b, c], partner)
+
+    own = pltpu.make_async_copy(mine, every.at[core, z, y, x], own_sem)
+    old_copy = remote(old, other, old_sems.at[0], old_sems.at[1], partner)
+
+    def start(copies):
+        for copy in copies:
+            copy.start()
+
+    def line_copies(zz, src_of):
+        return [copy for k in range(2) for copy in line_sends(k, zz, src_of(k))]
+
+    mine_of = lambda k: mine.at[:, colour[k]]
+    held_of = lambda zz: lambda k: block(k, zz, y, x)
+
+    @pl.when(z > 0)
+    def _():
+        start([downward(k, z, mine_of(k)) for k in range(2)])
+
+    @pl.when(z < deep - 1)
+    def _():
+        start([upward(k, z, mine_of(k)) for k in range(2)])
+
+    start(line_copies(z, mine_of))
+    own.start()
+    start([across(z, y, x, mine), old_copy])
+
+    def lines_at(t):
+        if t == 0:
+            return [(z, None, None)]
+        return [
+            (z - t, z >= t, (upward, z < deep - 1)),
+            (z + t, z < deep - t, (downward, z > 0)),
+        ]
+
+    def guarded(test, body):
+        if test is None:
+            body()
+        else:
+            pl.when(test)(body)
+
+    def stage_line(t):
+        for zz, test, (go, further) in lines_at(t):
+
+            def body(zz=zz, go=go, further=further):
+                for k in range(2):
+                    await_block(block(k, zz, y, x), recv.at[k, zz, y, x])
+                    pl.when(further)(lambda k=k: go(k, zz, block(k, zz, y, x)).start())
+                    start(line_sends(k, zz, block(k, zz, y, x)))
+                across(zz, y, x).start()
+
+            guarded(test, body)
+
+    def stage_near(t):
+        for zz, test, _ in lines_at(t):
+
+            def body(zz=zz):
+                for k in range(2):
+                    for n, (b, c) in enumerate(near[k]):
+                        await_block(block(k, zz, b, c), recv.at[k, zz, b, c])
+                        start(onward(k, zz, n, b, c))
+                for k in range(2):
+                    for b, c in far[k]:
+                        await_block(block(k, zz, b, c), recv.at[k, zz, b, c])
+                        across(zz, b, c).start()
+
+            guarded(test, body)
+
+    corner = [(b, c) for b in around(y, high) for c in around(x, wide)]
+
+    def stage_far(t):
+        for zz, test, _ in lines_at(t):
+
+            def body(zz=zz):
+                for b, c in corner:
+                    for k in range(2):
+                        await_block(block(k, zz, b, c), recv.at[k, zz, b, c])
+                    across(zz, b, c).start()
+
+            guarded(test, body)
+
+    if deep == 4:
+        order = [z, z + 1 - 2 * lax.rem(z, 2), 2 - z // 2, 3 - 3 * (z // 2)]
+    else:
+        order = [z] + around(z, deep)
+    pivot = lax.broadcasted_iota(jnp.int32, (piv, slots * cells), 0).astype(F32) + 1.0
+    most = []
+
+    def put(i):
+        zz = order[i]
+        for b in range(high):
+            for c in range(wide):
+                ref = every.at[1 - core, zz, b, c]
+                remote(ref, ref, core_recv.at[zz, b, c], core_recv.at[zz, b, c], partner).wait_recv()
+        lines = [every[0, zz, b, c, slots - 1 : slots, :part] for b in range(high) for c in range(wide)]
+        most.append(functools.reduce(jnp.maximum, [v[:, part - LANES :] for v in lines]))
+        line = functools.reduce(jnp.add, [v[:, : slots * cells] for v in lines])
+        seats = jnp.where(pivot == line, 1.0, 0.0).astype(BF16)
+        for c in range(2):
+            hi, lo = split(every[c, zz].reshape(cells * slots, width))
+            hi, lo = dot(seats, hi), dot(seats, lo)
+            cut = slice(c * (piv // 2), (c + 1) * (piv // 2))
+            if i == 0:
+                hi_ref[c] = hi[:, :half].astype(BF16)
+                lo_ref[c] = lo[:, :half].astype(BF16)
+                gram_ref[:, cut] = hi[:, half:] + lo[:, half:]
+            else:
+                hi_ref[c] += hi[:, :half].astype(BF16)
+                lo_ref[c] += lo[:, :half].astype(BF16)
+                gram_ref[:, cut] += hi[:, half:] + lo[:, half:]
+
+    def keep_old():
+        old_hi_ref[core], old_lo_ref[core] = split(old[...])
+        old_copy.wait_recv()
+        old_hi_ref[1 - core], old_lo_ref[1 - core] = split(other[...])
+
+    for t in range(deep + 3):
+        if 1 <= t < deep:
+            stage_line(t)
+        if 0 <= t - 1 < deep:
+            stage_near(t - 1)
+        if 0 <= t - 2 < deep:
+            stage_far(t - 2)
+        if t == 1:
+            keep_old()
+        if t == 2:
+            own.wait()
+        if 0 <= t - 3 < deep:
+            put(t - 3)
+
+    most_ref[...] = jnp.broadcast_to(functools.reduce(jnp.maximum, most), most_ref.shape)
+    for s in range(piv // LANES):
+        here, upto = slice(s * LANES, (s + 1) * LANES), slice(0, (s + 1) * LANES)
+        both = [
+            dot_t((hi_ref[c, here], lo_ref[c, here]), (hi_ref[c, upto], lo_ref[c, upto])) for c in range(2)
+        ]
+        gram_ref[here, upto] -= both[0] + both[1]
+
+    old_copy.wait_send()
+
+    @pl.when(z > 0)
+    def _():
+        for k in range(2):
+            downward(k, z, mine_of(k)).wait_send()
+
+    @pl.when(z < deep - 1)
+    def _():
+        for k in range(2):
+            upward(k, z, mine_of(k)).wait_send()
+
+    for t in range(deep):
+        for zz, test, go in lines_at(t):
+
+            def body(zz=zz, go=go, t=t):
+                for k in range(2):
+                    src = mine_of(k) if t == 0 else block(k, zz, y, x)
+                    if t:
+                        pl.when(go[1])(lambda k=k: go[0](k, zz, block(k, zz, y, x)).wait_send())
+                    for copy in line_sends(k, zz, src):
+                        copy.wait_send()
+                    for n, (b, c) in enumerate(near[k]):
+                        for copy in onward(k, zz, n, b, c):
+                            copy.wait_send()
+                for b in range(high):
+                    for c in range(wide):
+                        across(zz, b, c).wait_send()
+
+            guarded(test, body)
+
+
+def gather(grid, pivots, ids, old, eri, slots):
+    deep, high, wide = grid
+    piv = eri.shape[1]
+    width = old.shape[1] + piv // 2
+    peers = max(high, wide)
+    sem = pltpu.SemaphoreType.DMA
+    wide_bf16 = jax.ShapeDtypeStruct((2, piv, old.shape[1]), BF16)
+    any_space = pl.BlockSpec(memory_space=pl.ANY)
+    return pl.pallas_call(
+        functools.partial(gather_kernel, grid),
+        out_shape=(
+            jax.ShapeDtypeStruct((piv, piv), F32),
+            wide_bf16,
+            wide_bf16,
+            jax.ShapeDtypeStruct((2, *old.shape), BF16),
+            jax.ShapeDtypeStruct((2, *old.shape), BF16),
+            jax.ShapeDtypeStruct((SUB, LANES), F32),
+        ),
+        in_specs=[VMEM, VMEM, any_space, any_space],
+        out_specs=[VMEM] * 6,
+        scratch_shapes=[
+            pltpu.VMEM(old.shape, F32),
+            pltpu.VMEM(old.shape, F32),
+            pltpu.VMEM(eri.shape, F32),
+            pltpu.VMEM((slots, width), F32),
+            pltpu.VMEM((2, deep, high, wide, slots, width), F32),
+            sem((2,)),
+            sem,
+            sem((2, 2, deep)),
+            sem((2, deep, max(peers - 1, 1))),
+            sem((2, deep, peers, max(peers - 1, 1))),
+            sem((deep, high, wide)),
+            sem((2, deep, high, wide)),
+            sem((deep, high, wide)),
+            sem((2,)),
+        ],
+        compiler_params=pltpu.CompilerParams(
+            collective_id=1, has_side_effects=True, vmem_limit_bytes=40 * 1024 * 1024
+        ),
+        name="gather",
+    )(pivots, ids, old, eri)
+
+
 def finish_kernel(
-    steps, chips, all_ref, own_ref, other_ref, eri_ref, diag_ref, panel_ref, new_ref,
-    work, old_hi, old_lo,
+    steps, gram_ref, hi_ref, lo_ref, old_hi_ref, old_lo_ref, eri_hbm, diag_ref, panel_hbm, new_ref,
+    gram, work, panel, sems,
+):
+    piv = gram.shape[0]
+    width = piv // steps
+    f = functools.partial(lax.dot_general, preferred_element_type=F32)
+    load = pltpu.make_async_copy(eri_hbm, work, sems.at[steps])
+    load.start()
+    gram[...] = gram_ref[...]
+    rows = [(hi_ref[c], lo_ref[c]) for c in range(2)]
+    old = [(old_hi_ref[c], old_lo_ref[c]) for c in range(2)]
+    load.wait()
+    ones = jnp.ones((SUB, width), BF16)
+    new = diag_ref[...]
+    stores = []
+    for s in range(steps):
+        at = slice(s * width, (s + 1) * width)
+        inv = split(inverse_factor(gram[at, at]))
+        later = [slice(t * width, (t + 1) * width) for t in range(s + 1, steps)]
+        below = [split(dot_t(split(gram[t, at]), inv)) for t in later]
+        for i, t in enumerate(later):
+            for u in range(i + 1):
+                gram[t, later[u]] -= dot_t(below[i], below[u])
+        if s == 0:
+            work[...] -= dot_t(old[0], rows[0]) + dot_t(old[1], rows[1])
+        own = dot_t(split(work[:, at]), inv)
+        panel[:, at] = own
+        stores.append(pltpu.make_async_copy(panel.at[:, at], panel_hbm.at[:, at], sems.at[s]))
+        stores[-1].start()
+        hi, lo = split(own * own)
+        new = new - (f(ones, hi, ROWS_T) + f(ones, lo, ROWS_T))[:1]
+        own = split(own)
+        for i, t in enumerate(later):
+            work[:, t] -= dot_t(own, below[i])
+    new_ref[...] = new
+    for store in stores:
+        store.wait()
+
+
+def finish(steps, gathered, eri, diagonal):
+    rows, piv = eri.shape
+    any_space = pl.BlockSpec(memory_space=pl.ANY)
+    panels, new = pl.pallas_call(
+        functools.partial(finish_kernel, steps),
+        out_shape=(
+            jax.ShapeDtypeStruct((rows, piv), F32),
+            jax.ShapeDtypeStruct((1, rows), F32),
+        ),
+        in_specs=[VMEM] * 5 + [any_space, VMEM],
+        out_specs=[any_space, VMEM],
+        scratch_shapes=[
+            pltpu.VMEM((piv, piv), F32),
+            pltpu.VMEM((rows, piv), F32),
+            pltpu.VMEM((rows, piv), F32),
+            pltpu.SemaphoreType.DMA((steps + 1,)),
+        ],
+        compiler_params=pltpu.CompilerParams(vmem_limit_bytes=24 * 1024 * 1024),
+        name="finish",
+    )(*gathered, eri, diagonal[None, :])
+    return panels, new[0]
+
+
+def place_kernel(line_ref, every_ref, out_ref):
+    pivot = lax.broadcasted_iota(jnp.int32, (out_ref.shape[2], line_ref.shape[1]), 0).astype(F32) + 1.0
+    seats = jnp.where(pivot == line_ref[...], 1.0, 0.0).astype(BF16)
+    dot = functools.partial(
+        lax.dot_general, dimension_numbers=(((1,), (0,)), ((), ())), preferred_element_type=F32
+    )
+
+    def put(i, carry):
+        hi, lo = split(every_ref[i // 2, i % 2])
+        out_ref[i // 2, i % 2] = dot(seats, hi) + dot(seats, lo)
+        return carry
+
+    lax.fori_loop(0, 4, put, 0)
+
+
+def place(line, every, piv):
+    return pl.pallas_call(
+        place_kernel,
+        out_shape=jax.ShapeDtypeStruct((2, 2, piv, every.shape[-1]), F32),
+        in_specs=[VMEM] * 2,
+        out_specs=VMEM,
+        compiler_params=pltpu.CompilerParams(vmem_limit_bytes=40 * 1024 * 1024),
+        name="place",
+    )(line, every)
+
+
+def rolled_inverse(a):
+    n = a.shape[0]
+    row = lax.broadcasted_iota(jnp.int32, (n, n), 0)
+    lane = lax.broadcasted_iota(jnp.int32, (n, n), 1)
+
+    def pivot(j, held):
+        a, w = held
+        of_row = lambda v: jnp.sum(jnp.where(row == j, v, 0.0), axis=0, keepdims=True)
+        column = jnp.sum(jnp.where(lane == j, a, 0.0), axis=1, keepdims=True)
+        root = lax.rsqrt(jnp.sum(jnp.where((row == j) & (lane == j), a, 0.0), keepdims=True))
+        m = jnp.where(row > j, column, 0.0) * (root * root)
+        return a - m * of_row(a), jnp.where(row == j, w * root, w - m * of_row(w))
+
+    return lax.fori_loop(0, n, pivot, (a, jnp.where(row == lane, 1.0, 0.0)))[1]
+
+
+def rolled_kernel(
+    steps, parts_ref, own_ref, other_ref, eri_ref, diag_ref, panel_ref, new_ref,
+    hi, lo, work, solved,
 ):
     rows, piv = eri_ref.shape
     width = piv // steps
-    part = all_ref.shape[3]
-    slots = all_ref.shape[2] // chips
     half = own_ref.shape[1]
     core = lax.axis_index("col")
-    f = functools.partial(lax.dot_general, preferred_element_type=F32)
-
-    line = [all_ref[0, 0, slots * i + slots - 1 : slots * (i + 1), :LANES] for i in range(chips)]
-    if chips < LANES:
-        line.append(jnp.zeros((LANES - chips, LANES), F32))
-    line = jnp.concatenate(line, axis=0)
-    held = jnp.transpose(line)
-    number = lax.broadcasted_iota(jnp.int32, (slots, piv), 1).astype(F32) + 1.0
-    place = jnp.concatenate(
-        [
-            jnp.where(jnp.broadcast_to(held[:slots, i : i + 1], (slots, piv)) == number, 1.0, 0.0)
-            for i in range(chips)
-        ],
-        axis=0,
-    ).astype(BF16)
     for c in range(2):
-        for k in range(2):
-            hi, lo = split(all_ref[c, k])
-            hi = f(place, hi, COLS_T)
-            lo = f(place, lo, COLS_T)
-            if k == 0:
-                old_hi[c, :, :part] = hi.astype(BF16)
-                old_lo[c, :, :part] = lo.astype(BF16)
-            else:
-                rest = half - part
-                old_hi[c, :, part:] = hi[:, :rest].astype(BF16)
-                old_lo[c, :, part:] = lo[:, :rest].astype(BF16)
-                eri = piv // 2
-                work[:piv, c * eri : (c + 1) * eri] = hi[:, rest:] + lo[:, rest:]
-    both = [(old_hi[c], old_lo[c]) for c in range(2)]
-    work[:piv, :] = work[:piv, :] - (dot_t(both[0], both[0]) + dot_t(both[1], both[1]))
-    mine = (old_hi[core], old_lo[core])
-    theirs = (old_hi[1 - core], old_lo[1 - core])
-    work[piv:, :] = eri_ref[...] - (
-        dot_t(split(own_ref[...]), mine) + dot_t(split(other_ref[...]), theirs)
-    )
+        both = jnp.concatenate([parts_ref[c, 0], parts_ref[c, 1]], axis=1)
+        hi[c], lo[c] = split(both[:, :half])
+        work[:piv, c * (piv // 2) : (c + 1) * (piv // 2)] = both[:, half:]
+    at_block = lambda b: pl.ds(pl.multiple_of(b * LANES, LANES), LANES)
+
+    def gram(b, carry):
+        at = at_block(b)
+        work[at, :] -= dot_t((hi[0, at], lo[0, at]), (hi[0], lo[0])) + dot_t((hi[1, at], lo[1, at]), (hi[1], lo[1]))
+        return carry
+
+    def reduce(b, carry):
+        at = at_block(b)
+        work[pl.ds(pl.multiple_of(piv + b * LANES, LANES), LANES), :] = eri_ref[at, :] - (
+            dot_t(split(own_ref[at, :]), (hi[core], lo[core]))
+            + dot_t(split(other_ref[at, :]), (hi[1 - core], lo[1 - core]))
+        )
+        return carry
+
+    lax.fori_loop(0, piv // LANES, gram, 0)
+    lax.fori_loop(0, rows // LANES, reduce, 0)
     new_ref[...] = diag_ref[...]
     ones = jnp.ones((SUB, width), BF16)
+    f = functools.partial(lax.dot_general, dimension_numbers=ROWS_T, preferred_element_type=F32)
 
     def step(s, carry):
         at = pl.ds(pl.multiple_of(s * width, width), width)
-        inv = split(inverse_factor(work[at, at]))
-        solved = dot_t(split(work[:, at]), inv)
-        own = solved[piv:]
+        inv = split(rolled_inverse(work[at, at]))
+
+        def solve(b, carry):
+            solved[at_block(b), :] = dot_t(split(work[at_block(b), at]), inv)
+            return carry
+
+        lax.fori_loop(0, (piv + rows) // LANES, solve, 0)
+        own = solved[piv:, :]
         panel_ref[:, at] = own
-        hi, lo = split(own * own)
-        new_ref[...] -= (f(ones, hi, ROWS_T) + f(ones, lo, ROWS_T))[:1]
-
-        @pl.when(s < steps - 1)
-        def _():
-            both = split(solved)
-            work[...] -= dot_t(both, (both[0][:piv], both[1][:piv]))
-
+        high, low = split(own * own)
+        new_ref[...] -= (f(ones, high) + f(ones, low))[:1]
+        above = split(solved[:piv, :])
+
+        def update(b, carry):
+            work[at_block(b), :] -= dot_t(split(solved[at_block(b), :]), above)
+            return carry
+
+        lax.fori_loop(0, (piv + rows) // LANES, update, 0)
         return carry
 
     lax.fori_loop(0, steps, step, 0)
 
 
-def finish(steps, chips, everything, own, other, eri, diagonal):
+def rolled(steps, parts, own, other, eri, diagonal):
     rows, piv = eri.shape
     panels, new = pl.pallas_call(
-        functools.partial(finish_kernel, steps, chips),
+        functools.partial(rolled_kernel, steps),
         out_shape=(
             jax.ShapeDtypeStruct((rows, piv), F32),
             jax.ShapeDtypeStruct((1, rows), F32),
@@ -376,13 +829,14 @@
         in_specs=[VMEM] * 5,
         out_specs=[VMEM] * 2,
         scratch_shapes=[
-            pltpu.VMEM((piv + rows, piv), F32),
             pltpu.VMEM((2, piv, own.shape[1]), BF16),
             pltpu.VMEM((2, piv, own.shape[1]), BF16),
+            pltpu.VMEM((piv + rows, piv), F32),
+            pltpu.VMEM((piv + rows, piv // steps), F32),
         ],
-        compiler_params=pltpu.CompilerParams(vmem_limit_bytes=56 * 1024 * 1024),
-        name="finish",
-    )(everything, own, other, eri, diagonal[None, :])
+        compiler_params=pltpu.CompilerParams(vmem_limit_bytes=40 * 1024 * 1024),
+        name="rolled",
+    )(parts, own, other, eri, diagonal[None, :])
     return panels, new[0]
 
 
@@ -405,42 +859,27 @@
     slots = slots_for(piv, chips)
     cap = slots - 1
     ids = row_ids.reshape(-1, LANES)
-
-    def gather(window):
-        mine = pack(jnp.full((1,), window, jnp.int32), pivots, ids, old_factor, eri_cols, slots)
-        everything, other = spread(grid, mine, old_factor)
-        return everything.reshape(2, 2, chips * slots, -1), other
-
-    def line_of(everything):
-        return everything[0, 0].reshape(chips, slots, -1)[:, slots - 1, :LANES]
-
-    everything, other = gather(0)
-    most = jnp.max(line_of(everything)[:, LANES - 1]).astype(jnp.int32)
-    windows = (most + cap - 1) // cap
-
-    def placed(everything):
-        number = line_of(everything)[:, :slots].reshape(-1)
-        one = lax.broadcasted_iota(jnp.int32, (piv, chips * slots), 0) + 1 == number[None, :].astype(jnp.int32)
-        filled = jnp.arange(chips * slots) % slots < cap
-        dot = functools.partial(jnp.einsum, "ps,abse->abpe", precision=lax.Precision.HIGHEST)
-        return dot(jnp.where(one & filled[None, :], 1.0, 0.0), everything)
-
-    def more(state):
-        _, everything = state
-        rows = lax.fori_loop(
-            1, windows, lambda w, rows: rows + placed(gather(w)[0]), placed(everything)
-        )
-        rows = jnp.pad(rows, ((0, 0), (0, 0), (0, chips * cap - piv), (0, 0)))
-        rows = rows.reshape(2, 2, chips, cap, -1)
-        number = jnp.arange(chips * cap) + 1
-        number = jnp.where(number <= piv, number, 0).reshape(chips, cap).astype(F32)
-        line = jnp.pad(number, ((0, 0), (0, rows.shape[-1] - cap)))
-        line = jnp.broadcast_to(line[None, None, :, None], (2, 2, chips, 1, rows.shape[-1]))
-        rows = jnp.concatenate([rows, line], axis=3)
-        return jnp.bool_(False), rows.reshape(everything.shape)
-
-    _, everything = lax.while_loop(lambda s: s[0], more, (windows > 1, everything))
-    return finish(steps, chips, everything, old_factor, other, eri_cols, residual_diag)
+    paged = pivots.reshape(-1, LANES)
+
+    *gathered, most = gather(grid, paged, ids, old_factor, eri_cols, slots)
+    panels, new = finish(steps, gathered, eri_cols, residual_diag)
+    def again(state):
+        windows = (most[0, 0].astype(jnp.int32) + cap - 1) // cap
+
+        def add(w, held):
+            mine = pack(jnp.full((1,), w, jnp.int32), paged, ids, old_factor, eri_cols, slots)
+            every, other = spread(grid, mine, old_factor)
+            every = every.reshape(2, 2, chips, slots, -1)
+            line = every[0, 0, :, slots - 1, :slots].at[:, cap].set(0.0).reshape(1, -1)
+            every = every.reshape(2, 2, chips * slots, -1)
+            return held[0] + place(line, every, piv), other
+
+        empty = jnp.zeros((2, 2, piv, (old_factor.shape[1] + piv // 2) // 2), F32)
+        parts, other = lax.fori_loop(0, windows, add, (empty, jnp.zeros_like(old_factor)))
+        return jnp.bool_(False), *rolled(steps, parts, old_factor, other, eri_cols, residual_diag)
+
+    _, panels, new = lax.while_loop(lambda s: s[0], again, (most[0, 0] > cap, panels, new))
+    return panels, new
 
 
 def solution(mesh):

time: 85.6 us -> 53.3 us (0.62)
  the two profiles are of different devices: /device:TPU:11 before, /device:TPU:0 now
where the time goes in v2:
time: 53.3 us; the launch traced here: 53 us
  Pallas kernels  51 us (96%)
  between operations  1.49 us (3%)
  local copies, waits for them, and re-layouts  0.56 us (1%)
    pallas_call x1, Pallas kernels, gather(): pl.pallas_call(functools.partial(gather_kernel, grid), out_shape=(jax.Sha...  33.8 us
    pallas_call x1, Pallas kernels, finish(): pl.pallas_call(functools.partial(finish_kernel, steps), out_shape=(jax.Sh...  17.2 us

profile of v2, /device:TPU:0, one launch (start us, length us, event | category | flops | bytes accessed | tf_op | source)
XLA Modules:
  0.0 53.0 jit_solution(6037622580876368876)
XLA Ops:
  0.6 33.8 %gather.1 = (f32[512,512]{1,0:T(8,128)S(1)}, bf16[2,512,512]{2,1,0:T(8,128)(2,1)S(1)}, bf16[2,512,512]{2,1,0:T(8,128)(2,1)S(1)}, bf16[2,512,512]{2,1,0:T(8,128)(...) custom-call(s32[4,128]{1,0:T(4,128)} %pivot_ref.1, s32[4,128]{1,0:T(4,128)} %bitcast.30, ...), custom_call_target="tpu_custom_call" | custom-call | tf_op jit(solution)/shard_map/gather/pallas_call | solution.py:623
  34.4 0.0 copy-start.3
  34.4 0.0 copy-start.4
  34.4 0.0 copy-start.5
  34.4 17.2 %finish.1 = (f32[512,512]{1,0:T(8,128)}, f32[1,512]{1,0:T(1,128)}) custom-call(f32[512,512]{1,0:T(8,128)S(1)} %get-tuple-element.205.gram_ref, bf16[2,512,512]{2,1,0:T(8,128)(2,1)S(1)} %get-tuple-element.206.hi_ref, bf16[2,512,512]{2,1,0:T(8,128)(2,1)S(1)} %get-tuple-element.207.lo_ref, bf16[2,512,512]{2,1,0:T(8,128)(2,1)S(1)} %get-tuple-element.208.old_hi_ref, ...), custom_call_target="tpu_custom_call" | custom-call | tf_op jit(solution)/shard_map/finish/pallas_call | solution.py:701
  51.7 0.5 %slice.32 = f32[1,1]{1,0:T(1,128)} slice(f32[8,128]{1,0:T(8,128)S(1)} %get-tuple-element.356), slice={[0:1], [0:1]} | slice | bytes 8 | tf_op jit(solution)/shard_map/slice | solution.py:881
  52.8 0.0 copy-done.3
  52.9 0.0 copy-done.4
  52.9 0.0 copy-done.5
  (1 shorter events, 0.0 us)
Async XLA Ops:
  34.4 18.5 %copy-start.3 = (s32[4,128]{1,0:T(4,128)S(1)}, s32[4,128]{1,0:T(4,128)}, u32[]{:S(2)}) copy-start(s32[4,128]{1,0:T(4,128)} %pivot_ref.1) | copy-start | bytes 6148
  34.4 18.4 %copy-start.4 = (s32[512]{0:T(512)S(1)}, s32[512]{0:T(512)}, u32[]{:S(2)}) copy-start(s32[512]{0:T(512)} %param.15) | copy-start | bytes 6148
  34.4 18.4 %copy-start.5 = (f32[512]{0:T(512)S(1)}, f32[512]{0:T(512)}, u32[]{:S(2)}) copy-start(f32[512]{0:T(512)} %param.13) | copy-start | bytes 6148

commit v3 on v2

--- a/solution.py
+++ b/solution.py
@@ -38,12 +38,12 @@
     over = lambda v, k: jnp.broadcast_to(v[k : k + 1, :], (SUB, n))
     columns = lambda v, j: [jnp.broadcast_to(v[:, j + k : j + k + 1], (SUB, n)) for k in range(SUB)]
     out = []
-    V = columns(M[0], 0)
+    V = [jnp.where(row >= 0, v, 0.0) for v in columns(M[0], 0)]
     for g in range(groups):
         j = SUB * g
         ahead = g + 1 < groups
         if ahead:
-            U = columns(M[g + 1], j)
+            U = [jnp.where(row >= 0, v, 0.0) for v in columns(M[g + 1], j)]
             N = columns(M[g + 1], j + SUB)
         here = (lane >= j) & (lane < j + SUB)
         M[g] = jnp.where(here, jnp.where(lane == row + j, 1.0, 0.0), M[g])
@@ -310,8 +310,8 @@
 
 def gather_kernel(
     grid, pivot_ref, ids_ref, old_hbm, eri_hbm,
-    gram_ref, hi_ref, lo_ref, old_hi_ref, old_lo_ref, most_ref,
-    old, other, eri, mine, every,
+    gram_ref, hi_ref, lo_ref, old_hi_ref, old_lo_ref, eri, most_ref,
+    old, other, mine, every,
     in_sems, own_sem, z_send, near_send, far_send, core_send, recv, core_recv, old_sems,
 ):
     deep, high, wide = grid
@@ -573,13 +573,6 @@
             put(t - 3)
 
     most_ref[...] = jnp.broadcast_to(functools.reduce(jnp.maximum, most), most_ref.shape)
-    for s in range(piv // LANES):
-        here, upto = slice(s * LANES, (s + 1) * LANES), slice(0, (s + 1) * LANES)
-        both = [
-            dot_t((hi_ref[c, here], lo_ref[c, here]), (hi_ref[c, upto], lo_ref[c, upto])) for c in range(2)
-        ]
-        gram_ref[here, upto] -= both[0] + both[1]
-
     old_copy.wait_send()
 
     @pl.when(z > 0)
@@ -628,14 +621,14 @@
             wide_bf16,
             jax.ShapeDtypeStruct((2, *old.shape), BF16),
             jax.ShapeDtypeStruct((2, *old.shape), BF16),
+            jax.ShapeDtypeStruct(eri.shape, F32),
             jax.ShapeDtypeStruct((SUB, LANES), F32),
         ),
         in_specs=[VMEM, VMEM, any_space, any_space],
-        out_specs=[VMEM] * 6,
+        out_specs=[VMEM] * 7,
         scratch_shapes=[
             pltpu.VMEM(old.shape, F32),
             pltpu.VMEM(old.shape, F32),
-            pltpu.VMEM(eri.shape, F32),
             pltpu.VMEM((slots, width), F32),
             pltpu.VMEM((2, deep, high, wide, slots, width), F32),
             sem((2,)),
@@ -656,18 +649,19 @@
 
 
 def finish_kernel(
-    steps, gram_ref, hi_ref, lo_ref, old_hi_ref, old_lo_ref, eri_hbm, diag_ref, panel_hbm, new_ref,
-    gram, work, panel, sems,
+    steps, cap, gram_ref, hi_ref, lo_ref, old_hi_ref, old_lo_ref, eri_ref, most_ref, diag_ref,
+    panel_hbm, new_ref, over_ref, gram, work, panel, sems,
 ):
     piv = gram.shape[0]
     width = piv // steps
     f = functools.partial(lax.dot_general, preferred_element_type=F32)
-    load = pltpu.make_async_copy(eri_hbm, work, sems.at[steps])
-    load.start()
-    gram[...] = gram_ref[...]
+    over_ref[0] = jnp.where(jnp.max(most_ref[...]) > cap, 1, 0)
     rows = [(hi_ref[c], lo_ref[c]) for c in range(2)]
     old = [(old_hi_ref[c], old_lo_ref[c]) for c in range(2)]
-    load.wait()
+    for s in range(steps):
+        here, upto = slice(s * width, (s + 1) * width), slice(0, (s + 1) * width)
+        both = [dot_t((v[0][here], v[1][here]), (v[0][upto], v[1][upto])) for v in rows]
+        gram[here, upto] = gram_ref[here, upto] - (both[0] + both[1])
     ones = jnp.ones((SUB, width), BF16)
     new = diag_ref[...]
     stores = []
@@ -680,7 +674,7 @@
             for u in range(i + 1):
                 gram[t, later[u]] -= dot_t(below[i], below[u])
         if s == 0:
-            work[...] -= dot_t(old[0], rows[0]) + dot_t(old[1], rows[1])
+            work[...] = eri_ref[...] - (dot_t(old[0], rows[0]) + dot_t(old[1], rows[1]))
         own = dot_t(split(work[:, at]), inv)
         panel[:, at] = own
         stores.append(pltpu.make_async_copy(panel.at[:, at], panel_hbm.at[:, at], sems.at[s]))
@@ -695,27 +689,28 @@
         store.wait()
 
 
-def finish(steps, gathered, eri, diagonal):
-    rows, piv = eri.shape
+def finish(steps, cap, gathered, diagonal):
+    rows, piv = gathered[5].shape
     any_space = pl.BlockSpec(memory_space=pl.ANY)
-    panels, new = pl.pallas_call(
-        functools.partial(finish_kernel, steps),
+    panels, new, over = pl.pallas_call(
+        functools.partial(finish_kernel, steps, cap),
         out_shape=(
             jax.ShapeDtypeStruct((rows, piv), F32),
             jax.ShapeDtypeStruct((1, rows), F32),
+            jax.ShapeDtypeStruct((1,), jnp.int32),
         ),
-        in_specs=[VMEM] * 5 + [any_space, VMEM],
-        out_specs=[any_space, VMEM],
+        in_specs=[VMEM] * 8,
+        out_specs=[any_space, VMEM, SMEM],
         scratch_shapes=[
             pltpu.VMEM((piv, piv), F32),
             pltpu.VMEM((rows, piv), F32),
             pltpu.VMEM((rows, piv), F32),
-            pltpu.SemaphoreType.DMA((steps + 1,)),
+            pltpu.SemaphoreType.DMA((steps,)),
         ],
         compiler_params=pltpu.CompilerParams(vmem_limit_bytes=24 * 1024 * 1024),
         name="finish",
-    )(*gathered, eri, diagonal[None, :])
-    return panels, new[0]
+    )(*gathered, diagonal[None, :])
+    return over[0], panels, new[0]
 
 
 def place_kernel(line_ref, every_ref, out_ref):
@@ -861,8 +856,9 @@
     ids = row_ids.reshape(-1, LANES)
     paged = pivots.reshape(-1, LANES)
 
-    *gathered, most = gather(grid, paged, ids, old_factor, eri_cols, slots)
-    panels, new = finish(steps, gathered, eri_cols, residual_diag)
+    gathered = gather(grid, paged, ids, old_factor, eri_cols, slots)
+    most = gathered[-1]
+    result = finish(steps, cap, gathered, residual_diag)
     def again(state):
         windows = (most[0, 0].astype(jnp.int32) + cap - 1) // cap
 
@@ -876,10 +872,9 @@
 
         empty = jnp.zeros((2, 2, piv, (old_factor.shape[1] + piv // 2) // 2), F32)
         parts, other = lax.fori_loop(0, windows, add, (empty, jnp.zeros_like(old_factor)))
-        return jnp.bool_(False), *rolled(steps, parts, old_factor, other, eri_cols, residual_diag)
-
-    _, panels, new = lax.while_loop(lambda s: s[0], again, (most[0, 0] > cap, panels, new))
-    return panels, new
+        return jnp.int32(0), *rolled(steps, parts, old_factor, other, eri_cols, residual_diag)
+
+    return lax.while_loop(lambda s: s[0] > 0, again, result)[1:]
 
 
 def solution(mesh):

time: 53.3 us -> 48.3 us (0.906)
  Pallas kernels: 51 us -> 46.5 us
  loops' own time: 0.01 us -> 0.7 us
  between operations: 1.49 us -> 0.85 us
  local copies, waits for them, and re-layouts: 0.56 us -> 0.02 us
    pallas_call x1, Pallas kernels: 33.8 us -> 31.3 us  [gather(): pl.pallas_call(functools.partial(gather_kernel, grid), out_shape=(jax.Sha...]
    pallas_call x1, Pallas kernels: 17.2 us -> 15.2 us  [finish(): pl.pallas_call(functools.partial(finish_kernel, steps, cap), out_shape=(j...]
    another operation x1, loops' own time: 0.01 us -> 0.7 us  [on_device(): return lax.while_loop(lambda s: s[0] > 0, again, result)[1:]]
    slice x1 -> x0, local copies, waits for them, and re-layouts: 0.54 us -> none  [on_device(): most[0, 0] > cap]
where the time goes in v3:
time: 48.3 us; the launch traced here: 48.1 us
  Pallas kernels  46.5 us (96%)
  between operations  0.85 us (2%)
  loops' own time  0.7 us (1%)
    pallas_call x1, Pallas kernels, gather(): pl.pallas_call(functools.partial(gather_kernel, grid), out_shape=(jax.Sha...  31.3 us
    pallas_call x1, Pallas kernels, finish(): pl.pallas_call(functools.partial(finish_kernel, steps, cap), out_shape=(j...  15.2 us

profile of v3, /device:TPU:0, one launch (start us, length us, event | category | flops | bytes accessed | tf_op | source)
XLA Modules:
  0.0 48.1 jit_solution(9767322910756909179)
XLA Ops:
  0.6 31.3 %gather.1 = (f32[512,512]{1,0:T(8,128)S(1)}, bf16[2,512,512]{2,1,0:T(8,128)(2,1)S(1)}, bf16[2,512,512]{2,1,0:T(8,128)(2,1)S(1)}, bf16[2,512,512]{2,1,0:T(8,128)(...) custom-call(s32[4,128]{1,0:T(4,128)} %pivot_ref.1, s32[4,128]{1,0:T(4,128)} %bitcast.30, ...), custom_call_target="tpu_custom_call" | custom-call | tf_op jit(solution)/shard_map/gather/pallas_call | solution.py:616
  31.9 0.0 copy-start.3
  32.0 0.0 copy-start.4
  32.0 0.0 copy-start.5
  32.0 15.2 %finish.1 = (f32[512,512]{1,0:T(8,128)}, f32[1,512]{1,0:T(1,128)}, s32[1]{0:T(128)}) custom-call(f32[512,512]{1,0:T(8,128)S(1)} %get-tuple-element.206.gram_ref, bf16[2,512,512]{2,1,0:T(8,128)(2,1)S(1)} %get-tuple-element.207.hi_ref, bf16[2,512,512]{2,1,0:T(8,128)(2,1)S(1)} %get-tuple-element.208.lo_ref, ...), custom_call_target="tpu_custom_call" | custom-call | tf_op jit(solution)/shard_map/finish/pallas_call | solution.py:695
  47.2 0.0 copy-done.3
  47.2 0.0 copy-done.4
  47.2 0.0 copy-done.5
  47.2 0.7 %while.26 = (s32[]{:T(128)}, f32[512,512]{1,0:T(8,128)}, f32[512]{0:T(512)}, f32[8,128]{1,0:T(8,128)S(1)}, s32[4,128]{1,0:T(4,128)S(1)}, /*index=5*/s32[4,128]{1...) while((s32[]{:T(128)}, f32[512,512]{1,0:T(8,128)}, ...), condition=%region_4.5_spmd, body=%region_0.4_spmd | while | flops 786466 | bytes 51983512 | solution.py:877
Async XLA Ops:
  31.9 15.2 %copy-start.3 = (s32[4,128]{1,0:T(4,128)S(1)}, s32[4,128]{1,0:T(4,128)}, u32[]{:S(2)}) copy-start(s32[4,128]{1,0:T(4,128)} %pivot_ref.1) | copy-start | bytes 6148
  32.0 15.2 %copy-start.4 = (s32[512]{0:T(512)S(1)}, s32[512]{0:T(512)}, u32[]{:S(2)}) copy-start(s32[512]{0:T(512)} %param.15) | copy-start | bytes 6148
  32.0 15.2 %copy-start.5 = (f32[512]{0:T(512)S(1)}, f32[512]{0:T(512)}, u32[]{:S(2)}) copy-start(f32[512]{0:T(512)} %param.13) | copy-start | bytes 6148

commit v4 on v3

--- a/solution.py
+++ b/solution.py
@@ -45,10 +45,13 @@
         if ahead:
             U = [jnp.where(row >= 0, v, 0.0) for v in columns(M[g + 1], j)]
             N = columns(M[g + 1], j + SUB)
+        second = g + 2 < groups
+        if second:
+            U2 = [jnp.where(row >= 0, v, 0.0) for v in columns(M[g + 2], j)]
         here = (lane >= j) & (lane < j + SUB)
         M[g] = jnp.where(here, jnp.where(lane == row + j, 1.0, 0.0), M[g])
-        if ahead:
-            M[g + 1] = jnp.where(here, 0.0, M[g + 1])
+        for i in range(g + 1, min(g + 3, groups)):
+            M[i] = jnp.where(here, 0.0, M[i])
         roots = jnp.zeros((SUB, n), F32)
         invs = jnp.zeros((SUB, n), F32)
         for k in range(SUB):
@@ -70,15 +73,20 @@
                 M[g + 1] = M[g + 1] - u * r
                 for l in range(SUB):
                     N[l] = N[l] - u * over(U[k], l)
+            if second:
+                u = U2[k] * inv
+                for l in range(k + 1, SUB):
+                    U2[l] = U2[l] - u * top[l]
+                M[g + 2] = M[g + 2] - u * r
         out.append(jnp.where(lane < j + SUB, M[g] * roots, 0.0))
         if not ahead:
             break
-        if g + 2 < groups:
+        if g + 3 < groups:
             S = M[g] * invs
             for i in reversed(range(1, SUB)):
                 S = S - (jnp.where(row < i, V[i], 0.0) * invs) * over(S, i)
             S = [over(S, k) for k in range(SUB)]
-            for i in range(g + 2, groups):
+            for i in range(g + 3, groups):
                 C = columns(M[i], j)
                 M[i] = jnp.where(here, 0.0, M[i])
                 for k in range(SUB):
@@ -309,10 +317,10 @@
 
 
 def gather_kernel(
-    grid, pivot_ref, ids_ref, old_hbm, eri_hbm,
-    gram_ref, hi_ref, lo_ref, old_hi_ref, old_lo_ref, eri, most_ref,
+    grid, pivot_ref, ids_ref, old_hbm, eri_hbm, diag_hbm,
+    gram_ref, hi_ref, lo_ref, old_hi_ref, old_lo_ref, eri, most_ref, diag,
     old, other, mine, every,
-    in_sems, own_sem, z_send, near_send, far_send, core_send, recv, core_recv, old_sems,
+    in_sems, own_sem, z_send, cell_send, near_send, far_send, core_send, recv, core_recv, old_sems,
 ):
     deep, high, wide = grid
     cells = high * wide
@@ -347,6 +355,7 @@
     loads = [
         pltpu.make_async_copy(old_hbm, old, in_sems.at[0]),
         pltpu.make_async_copy(eri_hbm, eri, in_sems.at[1]),
+        pltpu.make_async_copy(diag_hbm, diag, in_sems.at[2]),
     ]
     for load in loads:
         load.start()
@@ -402,7 +411,8 @@
     ends = (z + deep - 1) // deep + (2 * deep - 2 - z) // deep
     pl.semaphore_wait(barrier, len(beside) + 1 + ends)
 
-    colour = [slice(0, part), slice(part, width)]
+    last = width - LANES
+    colour = [slice(0, part), slice(part, last), slice(last, width)]
 
     def block(k, zz, b, c):
         return every.at[core, zz, b, c, :, colour[k]]
@@ -416,14 +426,23 @@
     def await_block(ref, sem):
         remote(ref, ref, sem, sem, partner).wait_recv()
 
-    near = [[(y, o) for o in around(x, wide)], [(o, x) for o in around(y, high)]]
-    far = [near[1], near[0]]
+    aside = lambda o, along: (lax.rem(y + o * (1 - along), high), lax.rem(x + o * along, wide))
+    near = [[aside(o, 1 - core) for o in range(1, wide)], [aside(o, core) for o in range(1, wide)]]
+    near.append(near[0])
+    far = [near[1], near[0], near[1]]
 
     def upward(k, zz, src):
         return remote(src, block(k, zz, y, x), z_send.at[k, 0, zz], recv.at[k, zz, y, x], chip(z + 1, y, x))
 
     def downward(k, zz, src):
         return remote(src, block(k, zz, y, x), z_send.at[k, 1, zz], recv.at[k, zz, y, x], chip(z - 1, y, x))
+
+    def cell_on(way, zz, b, c, src=None):
+        ref = block(2, zz, b, c)
+        return remote(
+            ref if src is None else src, ref, cell_send.at[way, zz, b, c], recv.at[2, zz, b, c],
+            chip(z - 1 if way else z + 1, y, x),
+        )
 
     def line_sends(k, zz, src):
         out = []
@@ -457,6 +476,8 @@
     mine_of = lambda k: mine.at[:, colour[k]]
     held_of = lambda zz: lambda k: block(k, zz, y, x)
 
+    start(line_sends(2, z, mine_of(2)))
+
     @pl.when(z > 0)
     def _():
         start([downward(k, z, mine_of(k)) for k in range(2)])
@@ -473,8 +494,8 @@
         if t == 0:
             return [(z, None, None)]
         return [
-            (z - t, z >= t, (upward, z < deep - 1)),
-            (z + t, z < deep - t, (downward, z > 0)),
+            (z - t, z >= t, (upward, z < deep - 1, 0)),
+            (z + t, z < deep - t, (downward, z > 0, 1)),
         ]
 
     def guarded(test, body):
@@ -483,15 +504,48 @@
         else:
             pl.when(test)(body)
 
+    corner = [(b, c) for b in around(y, high) for c in around(x, wide)]
+    everywhere = [(b, c) for b in range(high) for c in range(wide)]
+
+    def stage_plane():
+        for n, (b, c) in enumerate(near[2]):
+            await_block(block(2, z, b, c), recv.at[2, z, b, c])
+            start(onward(2, z, n, b, c))
+
+    def stage_cells(t):
+        if t == 0:
+            for b, c in far[2] + corner:
+                await_block(block(2, z, b, c), recv.at[2, z, b, c])
+
+            @pl.when(z > 0)
+            def _():
+                start([cell_on(1, z, y, x, mine_of(2))] + [cell_on(1, z, b, c) for b, c in near[2] + far[2] + corner])
+
+            @pl.when(z < deep - 1)
+            def _():
+                start([cell_on(0, z, y, x, mine_of(2))] + [cell_on(0, z, b, c) for b, c in near[2] + far[2] + corner])
+
+            return
+        for zz, test, step in lines_at(t):
+
+            def body(zz=zz, step=step):
+                _, further, way = step
+                for b, c in everywhere:
+                    await_block(block(2, zz, b, c), recv.at[2, zz, b, c])
+                    pl.when(further)(lambda b=b, c=c: cell_on(way, zz, b, c).start())
+                across(zz, y, x).start()
+
+            guarded(test, body)
+
     def stage_line(t):
-        for zz, test, (go, further) in lines_at(t):
-
-            def body(zz=zz, go=go, further=further):
+        for zz, test, step in lines_at(t):
+
+            def body(zz=zz, step=step):
+                go, further, _ = step
                 for k in range(2):
                     await_block(block(k, zz, y, x), recv.at[k, zz, y, x])
                     pl.when(further)(lambda k=k: go(k, zz, block(k, zz, y, x)).start())
                     start(line_sends(k, zz, block(k, zz, y, x)))
-                across(zz, y, x).start()
 
             guarded(test, body)
 
@@ -509,8 +563,6 @@
                         across(zz, b, c).start()
 
             guarded(test, body)
-
-    corner = [(b, c) for b in around(y, high) for c in around(x, wide)]
 
     def stage_far(t):
         for zz, test, _ in lines_at(t):
@@ -553,59 +605,73 @@
                 lo_ref[c] += lo[:, :half].astype(BF16)
                 gram_ref[:, cut] += hi[:, half:] + lo[:, half:]
 
-    def keep_old():
-        old_hi_ref[core], old_lo_ref[core] = split(old[...])
-        old_copy.wait_recv()
-        old_hi_ref[1 - core], old_lo_ref[1 - core] = split(other[...])
-
+    stage_plane()
+    old_hi_ref[core], old_lo_ref[core] = split(old[...])
     for t in range(deep + 3):
         if 1 <= t < deep:
             stage_line(t)
         if 0 <= t - 1 < deep:
+            stage_cells(t - 1)
             stage_near(t - 1)
+        if t == 1:
+            old_copy.wait_recv()
+            old_hi_ref[1 - core], old_lo_ref[1 - core] = split(other[...])
+            own.wait()
+        if t == deep + 1:
+            for i in range(deep - 2):
+                put(i)
         if 0 <= t - 2 < deep:
             stage_far(t - 2)
-        if t == 1:
-            keep_old()
-        if t == 2:
-            own.wait()
-        if 0 <= t - 3 < deep:
-            put(t - 3)
+    for i in range(max(deep - 2, 0), deep):
+        put(i)
 
     most_ref[...] = jnp.broadcast_to(functools.reduce(jnp.maximum, most), most_ref.shape)
+    loads[2].wait()
     old_copy.wait_send()
+
+    def cells_sent(way, zz):
+        for b, c in everywhere:
+            cell_on(way, zz, b, c).wait_send()
 
     @pl.when(z > 0)
     def _():
         for k in range(2):
             downward(k, z, mine_of(k)).wait_send()
+        cells_sent(1, z)
 
     @pl.when(z < deep - 1)
     def _():
         for k in range(2):
             upward(k, z, mine_of(k)).wait_send()
+        cells_sent(0, z)
 
     for t in range(deep):
-        for zz, test, go in lines_at(t):
-
-            def body(zz=zz, go=go, t=t):
-                for k in range(2):
-                    src = mine_of(k) if t == 0 else block(k, zz, y, x)
-                    if t:
-                        pl.when(go[1])(lambda k=k: go[0](k, zz, block(k, zz, y, x)).wait_send())
+        for zz, test, step in lines_at(t):
+
+            def body(zz=zz, step=step, t=t):
+                if t:
+                    go, further, way = step
+
+                    @pl.when(further)
+                    def _():
+                        for k in range(2):
+                            go(k, zz, block(k, zz, y, x)).wait_send()
+                        cells_sent(way, zz)
+
+                for k in range(2 if t else 3):
+                    src = block(k, zz, y, x) if t else mine_of(k)
                     for copy in line_sends(k, zz, src):
                         copy.wait_send()
                     for n, (b, c) in enumerate(near[k]):
                         for copy in onward(k, zz, n, b, c):
                             copy.wait_send()
-                for b in range(high):
-                    for c in range(wide):
-                        across(zz, b, c).wait_send()
+                for b, c in everywhere:
+                    across(zz, b, c).wait_send()
 
             guarded(test, body)
 
 
-def gather(grid, pivots, ids, old, eri, slots):
+def gather(grid, pivots, ids, old, eri, diagonal, slots):
     deep, high, wide = grid
     piv = eri.shape[1]
     width = old.shape[1] + piv // 2
@@ -623,21 +689,23 @@
             jax.ShapeDtypeStruct((2, *old.shape), BF16),
             jax.ShapeDtypeStruct(eri.shape, F32),
             jax.ShapeDtypeStruct((SUB, LANES), F32),
+            jax.ShapeDtypeStruct((1, eri.shape[0]), F32),
         ),
-        in_specs=[VMEM, VMEM, any_space, any_space],
-        out_specs=[VMEM] * 7,
+        in_specs=[VMEM, VMEM] + [any_space] * 3,
+        out_specs=[VMEM] * 8,
         scratch_shapes=[
             pltpu.VMEM(old.shape, F32),
             pltpu.VMEM(old.shape, F32),
             pltpu.VMEM((slots, width), F32),
             pltpu.VMEM((2, deep, high, wide, slots, width), F32),
-            sem((2,)),
+            sem((3,)),
             sem,
             sem((2, 2, deep)),
-            sem((2, deep, max(peers - 1, 1))),
-            sem((2, deep, peers, max(peers - 1, 1))),
+            sem((2, deep, high, wide)),
+            sem((3, deep, max(peers - 1, 1))),
+            sem((3, deep, peers, max(peers - 1, 1))),
             sem((deep, high, wide)),
-            sem((2, deep, high, wide)),
+            sem((3, deep, high, wide)),
             sem((deep, high, wide)),
             sem((2,)),
         ],
@@ -645,12 +713,12 @@
             collective_id=1, has_side_effects=True, vmem_limit_bytes=40 * 1024 * 1024
         ),
         name="gather",
-    )(pivots, ids, old, eri)
+    )(pivots, ids, old, eri, diagonal[None, :])
 
 
 def finish_kernel(
     steps, cap, gram_ref, hi_ref, lo_ref, old_hi_ref, old_lo_ref, eri_ref, most_ref, diag_ref,
-    panel_hbm, new_ref, over_ref, gram, work, panel, sems,
+    panel_hbm, new_hbm, over_ref, gram, work, panel, new_ref, sems,
 ):
     piv = gram.shape[0]
     width = piv // steps
@@ -685,11 +753,13 @@
         for i, t in enumerate(later):
             work[:, t] -= dot_t(own, below[i])
     new_ref[...] = new
+    stores.append(pltpu.make_async_copy(new_ref, new_hbm, sems.at[steps]))
+    stores[-1].start()
     for store in stores:
         store.wait()
 
 
-def finish(steps, cap, gathered, diagonal):
+def finish(steps, cap, gathered):
     rows, piv = gathered[5].shape
     any_space = pl.BlockSpec(memory_space=pl.ANY)
     panels, new, over = pl.pallas_call(
@@ -700,16 +770,17 @@
             jax.ShapeDtypeStruct((1,), jnp.int32),
         ),
         in_specs=[VMEM] * 8,
-        out_specs=[any_space, VMEM, SMEM],
+        out_specs=[any_space, any_space, SMEM],
         scratch_shapes=[
             pltpu.VMEM((piv, piv), F32),
             pltpu.VMEM((rows, piv), F32),
             pltpu.VMEM((rows, piv), F32),
-            pltpu.SemaphoreType.DMA((steps,)),
+            pltpu.VMEM((1, rows), F32),
+            pltpu.SemaphoreType.DMA((steps + 1,)),
         ],
         compiler_params=pltpu.CompilerParams(vmem_limit_bytes=24 * 1024 * 1024),
         name="finish",
-    )(*gathered, diagonal[None, :])
+    )(*gathered)
     return over[0], panels, new[0]
 
 
@@ -856,9 +927,9 @@
     ids = row_ids.reshape(-1, LANES)
     paged = pivots.reshape(-1, LANES)
 
-    gathered = gather(grid, paged, ids, old_factor, eri_cols, slots)
-    most = gathered[-1]
-    result = finish(steps, cap, gathered, residual_diag)
+    gathered = gather(grid, paged, ids, old_factor, eri_cols, residual_diag, slots)
+    most = gathered[6]
+    result = finish(steps, cap, gathered)
     def again(state):
         windows = (most[0, 0].astype(jnp.int32) + cap - 1) // cap
 

time: 48.3 us -> 46.4 us (0.961)
  Pallas kernels: 46.5 us -> 44.6 us
    pallas_call x1, Pallas kernels: 31.3 us -> 30.3 us  [gather(): pl.pallas_call(functools.partial(gather_kernel, grid), out_shape=(jax.Sha...]
    pallas_call x1, Pallas kernels: 15.2 us -> 14.3 us  [finish(): pl.pallas_call(functools.partial(finish_kernel, steps, cap), out_shape=(j...]
where the time goes in v4:
time: 46.4 us; the launch traced here: 46.2 us
  Pallas kernels  44.6 us (96%)
  between operations  0.85 us (2%)
  loops' own time  0.7 us (2%)
    pallas_call x1, Pallas kernels, gather(): pl.pallas_call(functools.partial(gather_kernel, grid), out_shape=(jax.Sha...  30.3 us
    pallas_call x1, Pallas kernels, finish(): pl.pallas_call(functools.partial(finish_kernel, steps, cap), out_shape=(j...  14.3 us

profile of v4, /device:TPU:0, one launch (start us, length us, event | category | flops | bytes accessed | tf_op | source)
XLA Modules:
  0.0 46.2 jit_solution(15474880072598666102)
XLA Ops:
  0.6 30.3 %gather.1 = (f32[512,512]{1,0:T(8,128)S(1)}, bf16[2,512,512]{2,1,0:T(8,128)(2,1)S(1)}, bf16[2,512,512]{2,1,0:T(8,128)(2,1)S(1)}, bf16[2,512,512]{2,1,0:T(8,128)(...) custom-call(s32[4,128]{1,0:T(4,128)} %pivot_ref.1, ...), custom_call_target="tpu_custom_call" | custom-call | tf_op jit(solution)/shard_map/gather/pallas_call | solution.py:682
  31.0 0.0 copy-start.3
  31.0 0.0 copy-start.4
  31.0 0.0 copy-start.5
  31.0 14.3 %finish.1 = (f32[512,512]{1,0:T(8,128)}, f32[1,512]{1,0:T(1,128)}, s32[1]{0:T(128)}) custom-call(f32[512,512]{1,0:T(8,128)S(1)} %get-tuple-element.207.gram_ref, bf16[2,512,512]{2,1,0:T(8,128)(2,1)S(1)} %get-tuple-element.208.hi_ref, bf16[2,512,512]{2,1,0:T(8,128)(2,1)S(1)} %get-tuple-element.209.lo_ref, ...), custom_call_target="tpu_custom_call" | custom-call | tf_op jit(solution)/shard_map/finish/pallas_call | solution.py:765
  45.3 0.0 copy-done.3
  45.3 0.0 copy-done.4
  45.3 0.0 copy-done.5
  45.3 0.7 %while.26 = (s32[]{:T(128)}, f32[512,512]{1,0:T(8,128)}, f32[512]{0:T(512)}, f32[8,128]{1,0:T(8,128)S(1)}, s32[4,128]{1,0:T(4,128)S(1)}, /*index=5*/s32[4,128]{1...) while((s32[]{:T(128)}, f32[512,512]{1,0:T(8,128)}, ...), condition=%region_4.5_spmd, body=%region_0.4_spmd | while | flops 786466 | bytes 51983512 | solution.py:948
Async XLA Ops:
  31.0 14.3 %copy-start.3 = (s32[4,128]{1,0:T(4,128)S(1)}, s32[4,128]{1,0:T(4,128)}, u32[]{:S(2)}) copy-start(s32[4,128]{1,0:T(4,128)} %pivot_ref.1) | copy-start | bytes 6148
  31.0 14.3 %copy-start.4 = (s32[512]{0:T(512)S(1)}, s32[512]{0:T(512)}, u32[]{:S(2)}) copy-start(s32[512]{0:T(512)} %param.15) | copy-start | bytes 6148
  31.0 14.3 %copy-start.5 = (f32[512]{0:T(512)S(1)}, f32[512]{0:T(512)}, u32[]{:S(2)}) copy-start(f32[512]{0:T(512)} %param.13) | copy-start | bytes 6148

commit v5 on v4

--- a/solution.py
+++ b/solution.py
@@ -317,9 +317,9 @@
 
 
 def gather_kernel(
-    grid, pivot_ref, ids_ref, old_hbm, eri_hbm, diag_hbm,
+    grid, pivot_hbm, ids_hbm, old_hbm, eri_hbm, diag_hbm,
     gram_ref, hi_ref, lo_ref, old_hi_ref, old_lo_ref, eri, most_ref, diag,
-    old, other, mine, every,
+    pivot_ref, ids_ref, old, other, mine, every,
     in_sems, own_sem, z_send, cell_send, near_send, far_send, core_send, recv, core_recv, old_sems,
 ):
     deep, high, wide = grid
@@ -338,6 +338,16 @@
     chip = lambda z, y, x: ((z * high + y) * wide + x, core)
     around = lambda at, size: [lax.rem(at + o, size) for o in range(1, size)]
 
+    loads = [
+        pltpu.make_async_copy(old_hbm, old, in_sems.at[0]),
+        pltpu.make_async_copy(eri_hbm, eri, in_sems.at[1]),
+        pltpu.make_async_copy(diag_hbm, diag, in_sems.at[2]),
+        pltpu.make_async_copy(pivot_hbm, pivot_ref, in_sems.at[3]),
+        pltpu.make_async_copy(ids_hbm, ids_ref, in_sems.at[4]),
+    ]
+    for load in loads[3:] + loads[:3]:
+        load.start()
+
     barrier = pltpu.get_barrier_semaphore()
     signal = functools.partial(pl.semaphore_signal, barrier, inc=1, device_id_type=MESH)
     beside = [chip(z, o, x) for o in around(y, high)] + [chip(z, y, o) for o in around(x, wide)]
@@ -352,17 +362,11 @@
     def _():
         signal(device_id=chip(z + 1, y, x))
 
-    loads = [
-        pltpu.make_async_copy(old_hbm, old, in_sems.at[0]),
-        pltpu.make_async_copy(eri_hbm, eri, in_sems.at[1]),
-        pltpu.make_async_copy(diag_hbm, diag, in_sems.at[2]),
-    ]
-    for load in loads:
-        load.start()
-
     dot = functools.partial(
         lax.dot_general, dimension_numbers=(((1,), (0,)), ((), ())), preferred_element_type=F32
     )
+    loads[3].wait()
+    loads[4].wait()
     wanted = [
         jnp.transpose(jnp.broadcast_to(pivot_ref[b : b + 1].astype(F32), (LANES, LANES)))
         for b in range(pages)
@@ -691,14 +695,16 @@
             jax.ShapeDtypeStruct((SUB, LANES), F32),
             jax.ShapeDtypeStruct((1, eri.shape[0]), F32),
         ),
-        in_specs=[VMEM, VMEM] + [any_space] * 3,
+        in_specs=[any_space] * 5,
         out_specs=[VMEM] * 8,
         scratch_shapes=[
+            pltpu.VMEM(pivots.shape, jnp.int32),
+            pltpu.VMEM(ids.shape, jnp.int32),
             pltpu.VMEM(old.shape, F32),
             pltpu.VMEM(old.shape, F32),
             pltpu.VMEM((slots, width), F32),
             pltpu.VMEM((2, deep, high, wide, slots, width), F32),
-            sem((3,)),
+            sem((5,)),
             sem,
             sem((2, 2, deep)),
             sem((2, deep, high, wide)),

time: 46.4 us -> 45.8 us (0.987)
  Pallas kernels: 44.6 us -> 44 us
    pallas_call x1, Pallas kernels: 30.3 us -> 29.7 us  [gather(): pl.pallas_call(functools.partial(gather_kernel, grid), out_shape=(jax.Sha...]
where the time goes in v5:
time: 45.8 us; the launch traced here: 45.6 us
  Pallas kernels  44 us (96%)
  between operations  0.85 us (2%)
  loops' own time  0.7 us (2%)
    pallas_call x1, Pallas kernels, gather(): pl.pallas_call(functools.partial(gather_kernel, grid), out_shape=(jax.Sha...  29.7 us
    pallas_call x1, Pallas kernels, finish(): pl.pallas_call(functools.partial(finish_kernel, steps, cap), out_shape=(j...  14.3 us

profile of v5, /device:TPU:0, one launch (start us, length us, event | category | flops | bytes accessed | tf_op | source)
XLA Modules:
  0.0 45.6 jit_solution(2502747689971466791)
XLA Ops:
  0.6 29.7 %gather.1 = (f32[512,512]{1,0:T(8,128)S(1)}, bf16[2,512,512]{2,1,0:T(8,128)(2,1)S(1)}, bf16[2,512,512]{2,1,0:T(8,128)(2,1)S(1)}, bf16[2,512,512]{2,1,0:T(8,128)(...) custom-call(s32[4,128]{1,0:T(4,128)} %pivot_hbm.1, ...), custom_call_target="tpu_custom_call" | custom-call | tf_op jit(solution)/shard_map/gather/pallas_call | solution.py:686
  30.4 0.0 copy-start.3
  30.4 0.0 copy-start.4
  30.4 0.0 copy-start.5
  30.4 14.3 %finish.1 = (f32[512,512]{1,0:T(8,128)}, f32[1,512]{1,0:T(1,128)}, s32[1]{0:T(128)}) custom-call(f32[512,512]{1,0:T(8,128)S(1)} %get-tuple-element.207.gram_ref, bf16[2,512,512]{2,1,0:T(8,128)(2,1)S(1)} %get-tuple-element.208.hi_ref, bf16[2,512,512]{2,1,0:T(8,128)(2,1)S(1)} %get-tuple-element.209.lo_ref, ...), custom_call_target="tpu_custom_call" | custom-call | tf_op jit(solution)/shard_map/finish/pallas_call | solution.py:771
  44.7 0.0 copy-done.3
  44.7 0.0 copy-done.4
  44.7 0.0 copy-done.5
  44.7 0.7 %while.26 = (s32[]{:T(128)}, f32[512,512]{1,0:T(8,128)}, f32[512]{0:T(512)}, f32[8,128]{1,0:T(8,128)S(1)}, s32[4,128]{1,0:T(4,128)S(1)}, /*index=5*/s32[4,128]{1...) while((s32[]{:T(128)}, f32[512,512]{1,0:T(8,128)}, ...), condition=%region_4.5_spmd, body=%region_0.4_spmd | while | flops 786466 | bytes 51983512 | solution.py:954
Async XLA Ops:
  30.4 14.3 %copy-start.3 = (s32[4,128]{1,0:T(4,128)S(1)}, s32[4,128]{1,0:T(4,128)}, u32[]{:S(2)}) copy-start(s32[4,128]{1,0:T(4,128)} %pivot_hbm.1) | copy-start | bytes 6148
  30.4 14.3 %copy-start.4 = (s32[512]{0:T(512)S(1)}, s32[512]{0:T(512)}, u32[]{:S(2)}) copy-start(s32[512]{0:T(512)} %param.15) | copy-start | bytes 6148
  30.4 14.3 %copy-start.5 = (f32[512]{0:T(512)S(1)}, f32[512]{0:T(512)}, u32[]{:S(2)}) copy-start(f32[512]{0:T(512)} %param.13) | copy-start | bytes 6148

commit v6 on v5

--- a/solution.py
+++ b/solution.py
@@ -561,6 +561,13 @@
                     for n, (b, c) in enumerate(near[k]):
                         await_block(block(k, zz, b, c), recv.at[k, zz, b, c])
                         start(onward(k, zz, n, b, c))
+
+            guarded(test, body)
+
+    def stage_beside(t):
+        for zz, test, _ in lines_at(t):
+
+            def body(zz=zz):
                 for k in range(2):
                     for b, c in far[k]:
                         await_block(block(k, zz, b, c), recv.at[k, zz, b, c])
@@ -615,8 +622,9 @@
         if 1 <= t < deep:
             stage_line(t)
         if 0 <= t - 1 < deep:
+            stage_near(t - 1)
             stage_cells(t - 1)
-            stage_near(t - 1)
+            stage_beside(t - 1)
         if t == 1:
             old_copy.wait_recv()
             old_hi_ref[1 - core], old_lo_ref[1 - core] = split(other[...])

time: 45.8 us -> 45.3 us (0.989)
  no operation moved by 1% of the time
where the time goes in v6:
time: 45.3 us; the launch traced here: 45.2 us
  Pallas kernels  43.6 us (96%)
  between operations  0.85 us (2%)
  loops' own time  0.7 us (2%)
    pallas_call x1, Pallas kernels, gather(): pl.pallas_call(functools.partial(gather_kernel, grid), out_shape=(jax.Sha...  29.3 us
    pallas_call x1, Pallas kernels, finish(): pl.pallas_call(functools.partial(finish_kernel, steps, cap), out_shape=(j...  14.3 us

profile of v6, /device:TPU:0, one launch (start us, length us, event | category | flops | bytes accessed | tf_op | source)
XLA Modules:
  0.0 45.2 jit_solution(2623983780162491636)
XLA Ops:
  0.6 29.3 %gather.1 = (f32[512,512]{1,0:T(8,128)S(1)}, bf16[2,512,512]{2,1,0:T(8,128)(2,1)S(1)}, bf16[2,512,512]{2,1,0:T(8,128)(2,1)S(1)}, bf16[2,512,512]{2,1,0:T(8,128)(...) custom-call(s32[4,128]{1,0:T(4,128)} %pivot_hbm.1, ...), custom_call_target="tpu_custom_call" | custom-call | tf_op jit(solution)/shard_map/gather/pallas_call | solution.py:694
  29.9 0.0 copy-start.3
  29.9 0.0 copy-start.4
  30.0 0.0 copy-start.5
  30.0 14.3 %finish.1 = (f32[512,512]{1,0:T(8,128)}, f32[1,512]{1,0:T(1,128)}, s32[1]{0:T(128)}) custom-call(f32[512,512]{1,0:T(8,128)S(1)} %get-tuple-element.207.gram_ref, bf16[2,512,512]{2,1,0:T(8,128)(2,1)S(1)} %get-tuple-element.208.hi_ref, bf16[2,512,512]{2,1,0:T(8,128)(2,1)S(1)} %get-tuple-element.209.lo_ref, ...), custom_call_target="tpu_custom_call" | custom-call | tf_op jit(solution)/shard_map/finish/pallas_call | solution.py:779
  44.3 0.0 copy-done.3
  44.3 0.0 copy-done.4
  44.3 0.0 copy-done.5
  44.3 0.7 %while.26 = (s32[]{:T(128)}, f32[512,512]{1,0:T(8,128)}, f32[512]{0:T(512)}, f32[8,128]{1,0:T(8,128)S(1)}, s32[4,128]{1,0:T(4,128)S(1)}, /*index=5*/s32[4,128]{1...) while((s32[]{:T(128)}, f32[512,512]{1,0:T(8,128)}, ...), condition=%region_4.5_spmd, body=%region_0.4_spmd | while | flops 786466 | bytes 51983512 | solution.py:962
Async XLA Ops:
  29.9 14.3 %copy-start.3 = (s32[4,128]{1,0:T(4,128)S(1)}, s32[4,128]{1,0:T(4,128)}, u32[]{:S(2)}) copy-start(s32[4,128]{1,0:T(4,128)} %pivot_hbm.1) | copy-start | bytes 6148
  29.9 14.3 %copy-start.4 = (s32[512]{0:T(512)S(1)}, s32[512]{0:T(512)}, u32[]{:S(2)}) copy-start(s32[512]{0:T(512)} %param.15) | copy-start | bytes 6148
  30.0 14.3 %copy-start.5 = (f32[512]{0:T(512)S(1)}, f32[512]{0:T(512)}, u32[]{:S(2)}) copy-start(f32[512]{0:T(512)} %param.13) | copy-start | bytes 6148
